TPU v7x, 256 devices: a whole 4x4x8 slice. The times are simulated.
256 devices in a mesh: group: 4 (over y), dp: 8 (over z_lo, core), mp: 8 (over z_hi, x).
Axes of the slice: x: 4, y: 4, z: 8 (z_hi: 2, z_lo: 4; z = z_hi * 4 + z_lo), core: 2. Of those that a mesh axis runs over, the one named last changes fastest.
Arguments:
- patches: bfloat16 [1024, 12800], P(('group', 'mp'), 'dp'), may hold values from -6 to 6
- norm_gain: float32 [12800], P('dp'), may hold values from 0.25 to 1.75
- norm_bias: float32 [12800], P('dp'), may hold values from -3 to 3
- proj_in: bfloat16 [12800, 4096], P('dp', ('group', 'mp')), may hold values from -0.0546875 to 0.0546875
- proj_in_bias: float32 [4096], P(('group', 'mp')), may hold values from -3 to 3
- proj_out: bfloat16 [4096, 4096], P(('group', 'mp'), 'dp'), may hold values from -0.09375 to 0.09375
- proj_out_bias: float32 [4096], P('dp'), may hold values from -3 to 3
- text_rows: bfloat16 [1024, 4096], P(('group', 'mp'), 'dp'), may hold values from -6 to 6
- out_grads: bfloat16 [1024, 4096], P(('group', 'mp'), 'dp'), may hold values from -6 to 6
- gate_weight: bfloat16 [4096, 14336], P('dp', 'mp'), may hold values from -0.09375 to 0.09375
- up_weight: bfloat16 [4096, 14336], P('dp', 'mp'), may hold values from -0.09375 to 0.09375
- down_weight: bfloat16 [14336, 4096], P('mp', 'dp'), may hold values from -0.046875 to 0.046875
- image_counts: int32 [16], replicated, may hold values from 16 to 64, as said below
- image_sequence: int32 [16], replicated, may hold values from 0 to 7, as said below
- image_offsets: int32 [16], replicated, may hold values from 0 to 112, as said below
Outputs:
- projected: bfloat16 [1024, 4096], P(('group', 'mp'), 'dp')
- sequence_grads: bfloat16 [1024, 4096], P(('group', 'mp'), 'dp')
- row_grads: bfloat16 [1024, 4096], P(('group', 'mp'), 'dp')
Inputs may be any that keep to these rules, and one draw needn't show every extreme that they name: `image_counts`: image rows lie end to end from row 0 in image order; rows after the last image belong to no image. `image_sequence`: every sequence holds exactly two images. `image_offsets`: the two images of a sequence do not intersect and lie within its 128 rows.
All inputs are finite; a program needn't handle non-finite values.
Results may differ from a plain program's by a relative error of at most 0.0075.
Values may be sent and summed in bfloat16 or wider, within the bound.
No kernel may reach another device: no remote copies, remote signals or barrier semaphores. Data moves between devices by JAX's collectives and lax.ppermute only.
A program may use at most 64 MiB of HBM per device.

v0:
```python
import jax
import jax.numpy as jnp
from jax import lax
from jax.experimental import pallas as pl
from jax.experimental.pallas import tpu as pltpu
from jax.sharding import Mesh
from jax.sharding import PartitionSpec as P


TOK_DEV = 128
ROWS = ("g", "zh", "x")
DP = ("zl", "c")
MP = ("zh", "x")
BF = jnp.bfloat16
F32 = jnp.float32


def from_next(value, axis, k):
    n = lax.axis_size(axis)
    return lax.ppermute(value, axis, [((i + k) % n, i) for i in range(n)])


def swap(value, axis):
    return lax.ppermute(value, axis, [(0, 1), (1, 0)])


def copy_for_each(shard, axis):
    count = lax.axis_size(axis)
    return lax.all_to_all(
        jnp.broadcast_to(shard[None], (count, *shard.shape)), axis, 0, 0, tiled=True
    )


def in_order(own, other, index, dim=0):
    return jnp.where(
        index == 0,
        jnp.concatenate([own, other], axis=dim),
        jnp.concatenate([other, own], axis=dim),
    )


def mm(a, b):
    return jnp.dot(a, b, preferred_element_type=F32)


def mm_t(a, b):
    return lax.dot_general(a, b, (((1,), (1,)), ((), ())), preferred_element_type=F32)


def pick(onehot, rows):
    return mm(onehot, rows).astype(BF)


def three_parts(v):
    hi = lax.reduce_precision(v, 8, 7)
    mid = lax.reduce_precision(v - hi, 8, 7)
    low = v - hi - mid
    return jnp.stack([hi, mid, low]).astype(BF)


def seq_sources(counts, sequence, offsets, rows):
    starts = jnp.cumsum(counts) - counts
    seq = rows // TOK_DEV
    pos = rows % TOK_DEV
    hit = (
        (sequence[None, :] == seq[:, None])
        & (offsets[None, :] <= pos[:, None])
        & (pos[:, None] < (offsets + counts)[None, :])
    )
    source = jnp.sum(jnp.where(hit, starts[None, :] + pos[:, None] - offsets[None, :], 0), axis=1)
    return (source, jnp.any(hit, axis=1))


def image_targets(counts, sequence, offsets, rows):
    starts = jnp.cumsum(counts) - counts
    hit = (starts[None, :] <= rows[:, None]) & (rows[:, None] < (starts + counts)[None, :])
    target = jnp.sum(
        jnp.where(
            hit, sequence[None, :] * TOK_DEV + offsets[None, :] + rows[:, None] - starts[None, :], 0
        ),
        axis=1,
    )
    return (target, jnp.any(hit, axis=1))


def unit_grads(gate, up, hidden_grad):
    sig = jax.nn.sigmoid(gate)
    gate_grad = (hidden_grad * up * sig * (1.0 + gate * (1.0 - sig))).astype(BF)
    up_grad = (hidden_grad * gate * sig).astype(BF)
    return (gate_grad, up_grad)


def split3(v, axis=0):
    hi = lax.reduce_precision(v, 8, 7)
    mid = lax.reduce_precision(v - hi, 8, 7)
    return jnp.concatenate([hi, mid, v - hi - mid], axis=axis).astype(BF)


def row_share(whole, own):
    there = swap(whole[4 * own :], "c")
    near = whole[: 4 * own] + there
    sent = near[own:].astype(BF)
    total = near[:own]
    for k in (1, 2, 3):
        total = total + from_next(sent[own * (3 - k) : own * (4 - k)], "zl", k).astype(F32)
    return total


def first_kernel(c_ref, x_ref, gain_ref, bias_ref, w0, w1, w2, w3, keep_ref, send_ref, z_ref):
    count, feats = x_ref.shape
    units = w0.shape[1]
    half = 2 * units
    x = x_ref[...].astype(F32)
    mean = jnp.sum(x, axis=1, keepdims=True) * (1.0 / feats)
    centred = x - mean
    spread = jnp.sum(centred * centred, axis=1, keepdims=True) * (1.0 / feats)
    gain = gain_ref[...]
    z_ref[:count, :] = (centred * gain).astype(BF)
    bias = bias_ref[...]
    extra = []
    for v in (gain, bias):
        for _ in range(3):
            part = v.astype(BF).astype(F32)
            extra.append(part)
            v = v - part
    extra.append(jnp.zeros((10, feats), F32))
    z_ref[count:, :] = jnp.concatenate(extra, axis=0).astype(BF)
    lane = lax.broadcasted_iota(jnp.int32, (count, units), 1)
    stats = jnp.where(lane == 0, mean, jnp.where(lane == 1, spread, 0.0))
    for ref in (keep_ref, send_ref):
        ref[:count, half:] = stats
        ref[count:, half:] = jnp.zeros((16, units), F32)
    z = z_ref[...]
    low = c_ref[0] == 0
    for k, w in enumerate((w0, w1, w2, w3)):
        p = jnp.dot(z, w[...], preferred_element_type=F32)
        at = (k % 2) * units
        here, there = (keep_ref, send_ref) if k < 2 else (send_ref, keep_ref)

        @pl.when(low)
        def _():
            here[:, at : at + units] = p

        @pl.when(jnp.logical_not(low))
        def _():
            there[:, at : at + units] = p


VMEM = pl.BlockSpec(memory_space=pltpu.VMEM)
SMEM = pl.BlockSpec(memory_space=pltpu.SMEM)


def first_layer(rows, gain, bias, w_in, c_ref):
    count, feats = rows.shape
    units = w_in[0].shape[1]
    shape = (count + 16, 3 * units)
    return pl.pallas_call(
        first_kernel,
        out_shape=[jax.ShapeDtypeStruct(shape, F32)] * 2,
        in_specs=[SMEM] + [VMEM] * 7,
        out_specs=[VMEM, VMEM],
        scratch_shapes=[pltpu.VMEM((count + 16, feats), BF)],
        compiler_params=pltpu.CompilerParams(vmem_limit_bytes=32 << 20),
        cost_estimate=pl.CostEstimate(
            flops=2 * count * feats * 4 * units, bytes_accessed=4 << 20, transcendentals=0
        ),
        name="first_layer",
    )(c_ref, rows, gain.reshape(1, -1), bias.reshape(1, -1), *w_in)


def second_kernel(c_ref, own_ref, other_ref, w0, w1, w2, w3, out_ref):
    units = w0.shape[0] - 16
    ws = (w0, w1, w2, w3)
    low = c_ref[0] == 0
    for lead, cond in ((0, low), (2, jnp.logical_not(low))):

        @pl.when(cond)
        def _():
            total = jnp.zeros(out_ref.shape, F32)
            for j in range(4):
                act = own_ref if j < 2 else other_ref
                a = act[:, (j % 2) * units : (j % 2 + 1) * units]
                total += jnp.dot(a, ws[(lead + j) % 4][:units, :], preferred_element_type=F32)
            out_ref[...] = total.astype(out_ref.dtype)


def second_layer(own, other, w_out, c_ref):
    count = own.shape[0]
    cols = w_out[0].shape[1]
    return pl.pallas_call(
        second_kernel,
        out_shape=jax.ShapeDtypeStruct((count, cols), BF),
        in_specs=[SMEM] + [VMEM] * 6,
        out_specs=VMEM,
        compiler_params=pltpu.CompilerParams(vmem_limit_bytes=16 << 20),
        cost_estimate=pl.CostEstimate(
            flops=4 * count * own.shape[1] * cols, bytes_accessed=1 << 20, transcendentals=0
        ),
        name="second_layer",
    )(c_ref, own, other, *w_out)


def local(
    patches,
    norm_gain,
    norm_bias,
    proj_in,
    proj_in_bias,
    proj_out,
    proj_out_bias,
    text_rows,
    out_grads,
    gate_weight,
    up_weight,
    down_weight,
    image_counts,
    image_sequence,
    image_offsets,
):
    g, zl, c, zh, x = (lax.axis_index(a) for a in ("g", "zl", "c", "zh", "x"))
    units = proj_in.shape[1]
    width = gate_weight.shape[1]
    cols = text_rows.shape[1]
    feats = patches.shape[1]

    patch_other = swap(patches, "zh")
    w_in = [proj_in] + [from_next(proj_in, "g", k) for k in (1, 2, 3)]
    packed = jnp.concatenate(
        [proj_out, jnp.pad(three_parts(proj_in_bias), ((0, 13), (0, cols - units)))], axis=0
    )
    w_out = [packed] + [from_next(packed, "g", k) for k in (1, 2, 3)]
    pair = in_order(patches, patch_other, zh)
    rows = copy_for_each(pair, "x").reshape(-1, feats)
    count = rows.shape[0]
    own = count // 8

    side = jnp.concatenate([text_rows, out_grads], axis=1)
    side_other = swap(side, "zh")
    side_pair = in_order(side, side_other, zh)
    side_all = jnp.concatenate(
        [side_pair] + [from_next(side_pair, "x", k) for k in (1, 2, 3)], axis=0
    )
    text, cotangent = side_all[:, :cols], side_all[:, cols:]

    half = 2 * units
    c_ref = c.reshape(1).astype(jnp.int32)
    keep, send = first_layer(rows, norm_gain, norm_bias, w_in, c_ref)
    near = swap(send, "c")
    mean_a, spread_a = keep[:count, half : half + 1], keep[:count, half + 1 : half + 2]
    mean_b, spread_b = near[:count, half : half + 1], near[:count, half + 1 : half + 2]
    gain_a = jnp.sum(keep[count : count + 3, :half], axis=0, keepdims=True)
    gain_b = jnp.sum(near[count : count + 3, :half], axis=0, keepdims=True)
    shift = jnp.sum((keep + near)[count + 3 : count + 6, :half], axis=0, keepdims=True)
    apart = 0.5 * (mean_a - mean_b)
    mean = 0.5 * (mean_a + mean_b)
    spread = 0.5 * (spread_a + spread_b) + apart * apart
    summed = keep[:count, :half] + near[:count, :half] + apart * (gain_a - gain_b)
    tail = jnp.concatenate([split3(gain_a + gain_b), split3(shift)], axis=0)
    stats = jnp.concatenate([split3(mean, 1), split3(spread, 1)], axis=1)
    upper = jnp.concatenate([summed.astype(BF), jnp.pad(stats, ((0, 0), (0, units - 6)))], axis=1)
    lower = jnp.broadcast_to(jnp.pad(tail, ((0, 10), (0, units)))[None], (4, 16, half + units))
    message = jnp.concatenate([upper.reshape(4, count // 4, half + units), lower], axis=1)
    parts = lax.all_to_all(message, "zl", 0, 0, tiled=True).astype(F32)
    n = count // 4
    means = jnp.sum(parts[:, :n, half : half + 3], axis=2, keepdims=True)
    spreads = jnp.sum(parts[:, :n, half + 3 : half + 6], axis=2, keepdims=True)
    gains = jnp.sum(parts[:, n : n + 3, :half], axis=1, keepdims=True)
    shift = jnp.sum(parts[:, n + 3 : n + 6, :half], axis=(0, 1))
    mean = jnp.mean(means, axis=0, keepdims=True)
    spread = jnp.mean(spreads + (means - mean) * (means - mean), axis=0)
    total = jnp.sum(parts[:, :n, :half] + (means - mean) * gains, axis=0)
    bias = jnp.concatenate(
        [jnp.sum(w[units : units + 3, :units].astype(F32), axis=0) for w in w_out]
    )
    bias = jnp.where(c == 0, bias[:half], bias[half:])
    total = total * lax.rsqrt(spread + 1e-05) + (shift + bias)
    activated = jax.nn.gelu(total, approximate=False).astype(BF)
    act_own = copy_for_each(activated, "zl").reshape(count, half)
    act_other = swap(act_own, "c")

    second = second_layer(act_own, act_other, w_out, c_ref)
    parts = lax.all_to_all(second.reshape(4, count // 4, cols), "x", 0, 0, tiled=True)
    part = jnp.sum(parts.astype(F32), axis=0)
    part = part + swap(part.astype(BF), "zh").astype(F32)
    pair_projected = (part + proj_out_bias).astype(BF)
    projected = jnp.where(zh == 0, pair_projected[:own], pair_projected[own:])
    everything = copy_for_each(pair_projected, ("g", "x")).reshape(-1, cols)

    q = jnp.arange(count, dtype=jnp.int32)
    block = ((zl + (q // own) % 4) % 4) * 2 + (c + q // (4 * own)) % 2
    at = block * own + q % own
    source, covered = seq_sources(
        image_counts, image_sequence, image_offsets, g * count + at
    )

    def gathered_place(r):
        return (r // own) % 4 * (2 * own) + (r // (4 * own)) % 2 * own + r % own

    place = gathered_place(at)
    text_place = (place - x * (2 * own)) % count
    column = jnp.where(
        covered,
        source // count * count + gathered_place(source % count),
        everything.shape[0] + text_place,
    )
    choose = (column[:, None] == jnp.arange(everything.shape[0] + count)[None, :]).astype(BF)
    reorder = (text_place[:, None] == q[None, :]).astype(BF)
    inputs = pick(choose, jnp.concatenate([everything, text], axis=0))
    back_rows = pick(reorder, cotangent)

    hidden = mm_t(back_rows, down_weight)
    hidden_grad = row_share(hidden, own)
    whole = jnp.concatenate([mm(inputs, gate_weight), mm(inputs, up_weight)], axis=1)
    total = row_share(whole, own)
    gate_grad, up_grad = unit_grads(total[:, :width], total[:, width:], hidden_grad)

    grads = jnp.concatenate([gate_grad, up_grad], axis=1)
    line = jnp.concatenate([grads] + [from_next(grads, "zl", k) for k in (1, 2, 3)], axis=0)
    other = swap(line, "c")
    halves = [
        mm_t(h[:, :width], gate_weight) + mm_t(h[:, width:], up_weight) for h in (line, other)
    ]
    turned = jnp.concatenate(halves, axis=0).astype(BF)
    restore = (q[:, None] == place[None, :]).astype(BF)
    ordered = pick(restore, turned)
    parts = lax.all_to_all(ordered.reshape(4, count // 4, cols), "x", 0, 0, tiled=True)
    part = jnp.sum(parts.astype(F32), axis=0)
    pair_grads = (part + swap(part.astype(BF), "zh").astype(F32)).astype(BF)
    sequence_grads = jnp.where(zh == 0, pair_grads[:own], pair_grads[own:])

    column_rows = copy_for_each(pair_grads, "g").reshape(-1, cols)
    r = jnp.arange(4 * own, dtype=jnp.int32)
    target, valid = image_targets(
        image_counts, image_sequence, image_offsets, g * count + zh * (4 * own) + r
    )
    held = valid & ((target // own) % 4 == x)
    spot = target // count * (2 * own) + (target // (4 * own)) % 2 * own + target % own
    give = (held[:, None] & (spot[:, None] == q[None, :])).astype(BF)
    parts = lax.all_to_all(pick(give, column_rows).reshape(4, own, cols), "x", 0, 0, tiled=True)
    row_grads = jnp.sum(parts.astype(F32), axis=0).astype(BF)
    return (projected, sequence_grads, row_grads)


def solution(mesh):
    finer = Mesh(mesh.devices.reshape(4, 4, 2, 2, 4), ("g", "zl", "c", "zh", "x"))
    in_specs = (
        P(ROWS, DP),
        P(DP),
        P(DP),
        P(DP, ROWS),
        P(ROWS),
        P(ROWS, DP),
        P(DP),
        P(ROWS, DP),
        P(ROWS, DP),
        P(DP, MP),
        P(DP, MP),
        P(MP, DP),
        P(),
        P(),
        P(),
    )
    out_specs = (P(ROWS, DP), P(ROWS, DP), P(ROWS, DP))
    return jax.shard_map(local, mesh=finer, in_specs=in_specs, out_specs=out_specs, check_vma=False)
```

profile of v0, /device:TPU:32, one launch (start us, length us, event | category | flops | bytes accessed | tf_op | source)
XLA Modules:
  0.0 241.7 jit_solution(7790368855634214874)
XLA Ops:
  0.7 6.4 %collective-permute-start = (bf16[32,1600]{1,0:T(8,128)(2,1)}, bf16[32,1600]{1,0:T(8,128)(2,1)S(1)}, u32[]{:S(2)}, u32[]{:S(2)}) collective-permute-start(bf16[32,1600]{1,0:T(8,128)(2,1)} %param.15), channel_id=1, source_target_pairs={{0,4},{4,0},{1,5},{5,1},{2,6},{6,2},{3,7},{7,3},{8,12},{12,8},{9,1... | collective-permute-start | bytes 307208 | tf_op jit(solution)/shard_map/ppermute | solution.py:24
  7.1 5.5 %collective-permute-done = bf16[32,1600]{1,0:T(8,128)(2,1)S(1)} collective-permute-done((bf16[32,1600]{1,0:T(8,128)(2,1)}, bf16[32,1600]{1,0:T(8,128)(2,1)S(1)}, u32[]{:S(2)}, u32[]{:S(2)}) %collective-permute-start) | collective-permute-done | bytes 102432 | tf_op jit(solution)/shard_map/ppermute | solution.py:24
  12.6 1.0 maximum_select_fusion
  13.6 1.0 broadcast_in_dim.16
  14.6 4.4 %all-to-all-start = ((bf16[4,64,1600]{2,1,0:T(8,128)(2,1)}), bf16[4,64,1600]{2,1,0:T(8,128)(2,1)S(1)}, u32[]{:S(2)}, u32[]{:S(2)}) async-start(bf16[4,64,1600]{2,1,0:T(8,128)(2,1)} %broadcast_in_dim.16), calls=%async_computation | async-start | bytes 1703936 | tf_op jit(solution)/shard_map/all_to_all | solution.py:29
  19.0 3.0 %collective-permute-start.1 = (bf16[1600,128]{1,0:T(8,128)(2,1)S(1)}, bf16[1600,128]{1,0:T(8,128)(2,1)S(1)}, u32[]{:S(2)}, u32[]{:S(2)}) collective-permute-start(bf16[1600,128]{1,0:T(8,128)(2,1)S(1)} %copy-done.1), channel_id=1, source_target_pairs={{64,0},{128,64},{192,128},{0,192},{65,1},{129,65},{193,129},{1,193... | collective-permute-start | bytes 1228808 | tf_op jit(solution)/shard_map/ppermute | solution.py:20
  22.6 1.0 collective-permute-start.3
  23.6 12.7 %collective-permute-done.1.w1 = bf16[1600,128]{1,0:T(8,128)(2,1)S(1)} collective-permute-done((bf16[1600,128]{1,0:T(8,128)(2,1)S(1)}, bf16[1600,128]{1,0:T(8,128)(2,1)S(1)}, u32[]{:S(2)}, u32[]{:S(2)}) %collective-permute-start.1) | collective-permute-done | bytes 409632 | tf_op jit(solution)/shard_map/ppermute | solution.py:20
  37.1 3.1 %collective-permute-done.3.w3 = bf16[1600,128]{1,0:T(8,128)(2,1)} collective-permute-done((bf16[1600,128]{1,0:T(8,128)(2,1)S(1)}, bf16[1600,128]{1,0:T(8,128)(2,1)}, u32[]{:S(2)}, u32[]{:S(2)}) %collective-permute-start.3) | collective-permute-done | bytes 409632 | tf_op jit(solution)/shard_map/ppermute | solution.py:20
  40.1 1.0 copy-done.3
  41.1 4.2 %first_layer.1 = (f32[272,384]{1,0:T(8,128)S(1)}, f32[272,384]{1,0:T(8,128)S(1)}) custom-call(s32[1]{0:T(128)} %bitcast.c_ref, bf16[256,1600]{1,0:T(8,128)(2,1)S(1)} %bitcast.28, f32[1,1600]{1,0:T(1,128)S(1)} %reshape.808.gain_ref, f32[1,1600]{1,0:T(1,128)S(1)} %reshape.809.bias_ref, bf16[1600,128]{1,0:T(8,128)(2,1)S(1)} %copy-done.1, ...), custom_call_target="tpu_custom_call" | custom-call | flops 419430400 | bytes 4194304 | tf_op jit(solution)/shard_map/first_layer/pallas_call | solution.py:157
  46.2 1.4 collective-permute-start.7
  48.6 1.7 concatenate.76
  50.4 0.9 fusion.36
  52.0 6.4 %all-to-all-start.1 = ((bf16[4,80,384]{2,1,0:T(8,128)(2,1)}), bf16[4,80,384]{2,1,0:T(8,128)(2,1)S(1)}, u32[]{:S(2)}, u32[]{:S(2)}) async-start(bf16[4,80,384]{2,1,0:T(8,128)(2,1)} %pad_maximum_fusion.3), calls=%async_computation.1 | async-start | bytes 491520 | tf_op jit(solution)/shard_map/all_to_all | solution.py:263
  59.1 6.0 %collective-permute-done.6.w2 = bf16[144,512]{1,0:T(8,128)(2,1)S(1)} collective-permute-done((bf16[144,512]{1,0:T(8,128)(2,1)S(1)}, bf16[144,512]{1,0:T(8,128)(2,1)S(1)}, u32[]{:S(2)}, u32[]{:S(2)}) %collective-permute-start.6) | collective-permute-done | bytes 147488 | tf_op jit(solution)/shard_map/ppermute | solution.py:20
  66.1 9.9 %all_to_all.40 = bf16[4,64,256]{2,1,0:T(8,128)(2,1)S(1)} all-to-all(bf16[4,64,256]{2,1,0:T(8,128)(2,1)S(1)} %broadcast_in_dim.18), channel_id=1, replica_groups=mesh['g'=4,'zl'=4,'c'=2,'zh'=2,'x'=4] {'zl'}, dimensions={0} | all-to-all | bytes 262144 | tf_op jit(solution)/shard_map/all_to_all | solution.py:29
  76.0 1.3 collective-permute-done.8.other_ref
  77.3 1.1 second_layer.1
  78.4 4.5 %all-to-all-start.3 = ((bf16[4,64,512]{2,1,0:T(8,128)(2,1)}), bf16[4,64,512]{2,1,0:T(8,128)(2,1)S(1)}, u32[]{:S(2)}, u32[]{:S(2)}) async-start(bf16[4,64,512]{2,1,0:T(8,128)(2,1)} %bitcast.9), calls=%async_computation.3 | async-start | bytes 524288 | tf_op jit(solution)/shard_map/all_to_all | solution.py:282
  83.0 7.0 %all-to-all-done.3 = bf16[4,64,512]{2,1,0:T(8,128)(2,1)S(1)} async-done(((bf16[4,64,512]{2,1,0:T(8,128)(2,1)}), bf16[4,64,512]{2,1,0:T(8,128)(2,1)S(1)}, u32[]{:S(2)}, u32[]{:S(2)}) %all-to-all-start.3) | async-done | bytes 262176 | tf_op jit(solution)/shard_map/all_to_all | solution.py:282
  90.0 5.2 %collective-permute-start.9 = (bf16[64,512]{1,0:T(8,128)(2,1)S(1)}, bf16[64,512]{1,0:T(8,128)(2,1)S(1)}, u32[]{:S(2)}, u32[]{:S(2)}) collective-permute-start(bf16[64,512]{1,0:T(8,128)(2,1)S(1)} %convert_element_type.113), channel_id=1, source_target_pairs={{0,4},{4,0},{1,5},{5,1},{2,6},{6,2},{3,7},{7,3},{8,12},{12,8},{9,1... | collective-permute-start | bytes 196616 | tf_op jit(solution)/shard_map/ppermute | solution.py:24
  95.2 0.8 collective-permute-start.10
  96.3 2.8 %collective-permute-done.9 = bf16[64,512]{1,0:T(8,128)(2,1)S(1)} collective-permute-done((bf16[64,512]{1,0:T(8,128)(2,1)S(1)}, bf16[64,512]{1,0:T(8,128)(2,1)S(1)}, u32[]{:S(2)}, u32[]{:S(2)}) %collective-permute-start.9) | collective-permute-done | bytes 65568 | tf_op jit(solution)/shard_map/ppermute | solution.py:24
  99.1 1.1 broadcast_in_dim.20
  100.2 3.8 %all-to-all-start.4 = ((bf16[16,64,512]{2,1,0:T(8,128)(2,1)}), bf16[16,64,512]{2,1,0:T(8,128)(2,1)S(1)}, u32[]{:S(2)}, u32[]{:S(2)}) async-start(bf16[16,64,512]{2,1,0:T(8,128)(2,1)} %broadcast_in_dim.20), calls=%async_computation.4 | async-start | bytes 2097152 | tf_op jit(solution)/shard_map/all_to_all | solution.py:29
  104.3 2.2 collective-permute-start.13
  106.5 2.7 %collective-permute-start.12 = (bf16[64,1024]{1,0:T(8,128)(2,1)S(1)}, bf16[64,1024]{1,0:T(8,128)(2,1)S(1)}, u32[]{:S(2)}, u32[]{:S(2)}) collective-permute-start(bf16[64,1024]{1,0:T(8,128)(2,1)S(1)} %maximum_select_fusion.1), channel_id=1, source_target_pairs={{2,0},{3,1},{0,2},{1,3},{6,4},{7,5},{4,6},{5,7},{10,8},{11,9},{8,1... | collective-permute-start | bytes 393224 | tf_op jit(solution)/shard_map/ppermute | solution.py:20
  109.1 1.5 collective-permute-start.11
  110.7 10.0 %collective-permute-done.13 = bf16[64,1024]{1,0:T(8,128)(2,1)S(1)} collective-permute-done((bf16[64,1024]{1,0:T(8,128)(2,1)S(1)}, bf16[64,1024]{1,0:T(8,128)(2,1)S(1)}, u32[]{:S(2)}, u32[]{:S(2)}) %collective-permute-start.13) | collective-permute-done | bytes 131104 | tf_op jit(solution)/shard_map/ppermute | solution.py:20
  120.7 1.8 collective-permute-done.12
  123.2 1.5 fusion.6
  125.4 0.8 copy-done.4
  127.5 1.5 pad_maximum_fusion
  129.3 3.6 %fusion.9 = f32[256,1792]{1,0:T(8,128)} fusion(bf16[1792,512]{1,0:T(8,128)(2,1)} %param.26, bf16[256,1024]{1,0:T(8,128)(2,1)S(1)} %pad_maximum_fusion.2, s32[256]{0:T(256)S(1)} %get-tuple-element.20), kind=kOutput, calls=%fused_computation.15 | convolution fusion | flops 537067520 | bytes 3933184 | tf_op jit(solution)/shard_map/dot_general | solution.py:47
  132.9 1.4 slice.197
  134.9 2.1 collective-permute-done.14
  137.0 1.3 fusion.102
  138.3 1.8 fusion.103
  140.2 2.3 collective-permute-start.20
  142.6 2.1 collective-permute-start.17
  144.7 2.5 %collective-permute-start.16 = (bf16[32,1792]{1,0:T(8,128)(2,1)S(1)}, bf16[32,1792]{1,0:T(8,128)(2,1)S(1)}, u32[]{:S(2)}, u32[]{:S(2)}) collective-permute-start(bf16[32,1792]{1,0:T(8,128)(2,1)S(1)} %get-tuple-element.40), channel_id=1, source_target_pairs={{32,0},{48,16},{0,32},{16,48},{33,1},{49,17},{1,33},{17,49},{34,2}... | collective-permute-start | bytes 344072 | tf_op jit(solution)/shard_map/ppermute | solution.py:20
  147.2 1.5 collective-permute-done.21
  148.7 1.9 collective-permute-start.15
  150.6 15.3 %collective-permute-done.20 = bf16[32,3584]{1,0:T(8,128)(2,1)S(1)} collective-permute-done((bf16[32,3584]{1,0:T(8,128)(2,1)S(1)}, bf16[32,3584]{1,0:T(8,128)(2,1)S(1)}, u32[]{:S(2)}, u32[]{:S(2)}) %collective-permute-start.20) | collective-permute-done | bytes 229408 | tf_op jit(solution)/shard_map/ppermute | solution.py:20
  165.9 2.3 collective-permute-done.19
  168.4 2.1 collective-permute-done.16
  170.5 2.6 %collective-permute-done.15 = bf16[32,1792]{1,0:T(8,128)(2,1)S(1)} collective-permute-done((bf16[32,1792]{1,0:T(8,128)(2,1)S(1)}, bf16[32,1792]{1,0:T(8,128)(2,1)S(1)}, u32[]{:S(2)}, u32[]{:S(2)}) %collective-permute-start.15) | collective-permute-done | bytes 114720 | tf_op jit(solution)/shard_map/ppermute | solution.py:20
  173.4 1.4 collective-permute-start.23
  174.8 1.4 collective-permute-start.22
  176.2 5.6 %collective-permute-done.24 = bf16[32,3584]{1,0:T(8,128)(2,1)S(1)} collective-permute-done((bf16[32,3584]{1,0:T(8,128)(2,1)S(1)}, bf16[32,3584]{1,0:T(8,128)(2,1)S(1)}, u32[]{:S(2)}, u32[]{:S(2)}) %collective-permute-start.24) | collective-permute-done | bytes 229408 | tf_op jit(solution)/shard_map/ppermute | solution.py:20
  181.8 11.6 %collective-permute-done.23 = bf16[32,3584]{1,0:T(8,128)(2,1)S(1)} collective-permute-done((bf16[32,3584]{1,0:T(8,128)(2,1)S(1)}, bf16[32,3584]{1,0:T(8,128)(2,1)S(1)}, u32[]{:S(2)}, u32[]{:S(2)}) %collective-permute-start.23) | collective-permute-done | bytes 229408 | tf_op jit(solution)/shard_map/ppermute | solution.py:20
  193.4 1.6 collective-permute-done.22
  197.1 0.8 collective-permute-done.25
  199.3 0.9 convolution_convert_fusion
  200.3 3.4 %all-to-all-start.5 = ((bf16[4,64,512]{2,1,0:T(8,128)(2,1)}), bf16[4,64,512]{2,1,0:T(8,128)(2,1)S(1)}, u32[]{:S(2)}, u32[]{:S(2)}) async-start(bf16[4,64,512]{2,1,0:T(8,128)(2,1)} %bitcast.12), calls=%async_computation.5 | async-start | bytes 524288 | tf_op jit(solution)/shard_map/all_to_all | solution.py:326
  203.7 7.2 %all-to-all-done.5 = bf16[4,64,512]{2,1,0:T(8,128)(2,1)S(1)} async-done(((bf16[4,64,512]{2,1,0:T(8,128)(2,1)}), bf16[4,64,512]{2,1,0:T(8,128)(2,1)S(1)}, u32[]{:S(2)}, u32[]{:S(2)}) %all-to-all-start.5) | async-done | bytes 262176 | tf_op jit(solution)/shard_map/all_to_all | solution.py:326
  210.9 5.3 %collective-permute-start.26 = (bf16[64,512]{1,0:T(8,128)(2,1)S(1)}, bf16[64,512]{1,0:T(8,128)(2,1)S(1)}, u32[]{:S(2)}, u32[]{:S(2)}) collective-permute-start(bf16[64,512]{1,0:T(8,128)(2,1)S(1)} %convert_element_type.128), channel_id=1, source_target_pairs={{0,4},{4,0},{1,5},{5,1},{2,6},{6,2},{3,7},{7,3},{8,12},{12,8},{9,1... | collective-permute-start | bytes 196616 | tf_op jit(solution)/shard_map/ppermute | solution.py:24
  216.2 3.0 %collective-permute-done.26 = bf16[64,512]{1,0:T(8,128)(2,1)S(1)} collective-permute-done((bf16[64,512]{1,0:T(8,128)(2,1)S(1)}, bf16[64,512]{1,0:T(8,128)(2,1)S(1)}, u32[]{:S(2)}, u32[]{:S(2)}) %collective-permute-start.26) | collective-permute-done | bytes 65568 | tf_op jit(solution)/shard_map/ppermute | solution.py:24
  219.9 4.3 %all-to-all-start.6 = ((bf16[4,64,512]{2,1,0:T(8,128)(2,1)}), bf16[4,64,512]{2,1,0:T(8,128)(2,1)S(1)}, u32[]{:S(2)}, u32[]{:S(2)}) async-start(bf16[4,64,512]{2,1,0:T(8,128)(2,1)} %broadcast_in_dim.22), calls=%async_computation.6 | async-start | bytes 524288 | tf_op jit(solution)/shard_map/all_to_all | solution.py:29
  224.8 6.1 %all-to-all-done.6 = bf16[4,64,512]{2,1,0:T(8,128)(2,1)S(1)} async-done(((bf16[4,64,512]{2,1,0:T(8,128)(2,1)}), bf16[4,64,512]{2,1,0:T(8,128)(2,1)S(1)}, u32[]{:S(2)}, u32[]{:S(2)}) %all-to-all-start.6) | async-done | bytes 262176 | tf_op jit(solution)/shard_map/all_to_all | solution.py:29
  230.9 0.9 convolution_convert_fusion.2
  231.8 3.3 %all-to-all-start.7 = ((bf16[4,32,512]{2,1,0:T(8,128)(2,1)}), bf16[4,32,512]{2,1,0:T(8,128)(2,1)S(1)}, u32[]{:S(2)}, u32[]{:S(2)}) async-start(bf16[4,32,512]{2,1,0:T(8,128)(2,1)} %bitcast.14), calls=%async_computation.7 | async-start | bytes 262144 | tf_op jit(solution)/shard_map/all_to_all | solution.py:339
  235.7 5.3 %all-to-all-done.7 = bf16[4,32,512]{2,1,0:T(8,128)(2,1)S(1)} async-done(((bf16[4,32,512]{2,1,0:T(8,128)(2,1)}), bf16[4,32,512]{2,1,0:T(8,128)(2,1)S(1)}, u32[]{:S(2)}, u32[]{:S(2)}) %all-to-all-start.7) | async-done | bytes 131104 | tf_op jit(solution)/shard_map/all_to_all | solution.py:339
  (129 shorter events, 16.5 us)
Async XLA Ops:
  0.6 124.1 %copy-start = (bf16[512,1792]{1,0:T(8,128)(2,1)S(1)}, bf16[512,1792]{1,0:T(8,128)(2,1)}, u32[]{:S(2)}) copy-start(bf16[512,1792]{1,0:T(8,128)(2,1)} %param.25) | copy-start | bytes 5505028
  0.6 18.3 %copy-start.1 = (bf16[1600,128]{1,0:T(8,128)(2,1)S(1)}, bf16[1600,128]{1,0:T(8,128)(2,1)}, u32[]{:S(2)}) copy-start(bf16[1600,128]{1,0:T(8,128)(2,1)} %w0.1) | copy-start | bytes 1228804
  0.7 22.9 %copy-start.13 = (f32[1600]{0:T(1024)S(1)}, f32[1600]{0:T(1024)}, u32[]{:S(2)}) copy-start(f32[1600]{0:T(1024)} %param.16) | copy-start | bytes 19204
  0.7 22.9 %copy-start.14 = (f32[1600]{0:T(1024)S(1)}, f32[1600]{0:T(1024)}, u32[]{:S(2)}) copy-start(f32[1600]{0:T(1024)} %param.17) | copy-start | bytes 19204
  0.7 11.9 %collective-permute-start = (bf16[32,1600]{1,0:T(8,128)(2,1)}, bf16[32,1600]{1,0:T(8,128)(2,1)S(1)}, u32[]{:S(2)}, u32[]{:S(2)}) collective-permute-start(bf16[32,1600]{1,0:T(8,128)(2,1)} %param.15), channel_id=1, source_target_pairs={{0,4},{4,0},{1,5},{5,1},{2,6},{6,2},{3,7},{7,3},{8,12},{12,8},{9,1... | collective-permute-start | bytes 307208 | tf_op jit(solution)/shard_map/ppermute | solution.py:24
  14.6 30.9 %copy-start.19 = (f32[128]{0:T(128)S(1)}, f32[128]{0:T(128)}, u32[]{:S(2)}) copy-start(f32[128]{0:T(128)} %param.19) | copy-start | bytes 1540
  14.6 25.6 %all-to-all-start = ((bf16[4,64,1600]{2,1,0:T(8,128)(2,1)}), bf16[4,64,1600]{2,1,0:T(8,128)(2,1)S(1)}, u32[]{:S(2)}, u32[]{:S(2)}) async-start(bf16[4,64,1600]{2,1,0:T(8,128)(2,1)} %broadcast_in_dim.16), calls=%async_computation | async-start | bytes 1703936 | tf_op jit(solution)/shard_map/all_to_all | solution.py:29
  19.0 17.3 %collective-permute-start.1 = (bf16[1600,128]{1,0:T(8,128)(2,1)S(1)}, bf16[1600,128]{1,0:T(8,128)(2,1)S(1)}, u32[]{:S(2)}, u32[]{:S(2)}) collective-permute-start(bf16[1600,128]{1,0:T(8,128)(2,1)S(1)} %copy-done.1), channel_id=1, source_target_pairs={{64,0},{128,64},{192,128},{0,192},{65,1},{129,65},{193,129},{1,193... | collective-permute-start | bytes 1228808 | tf_op jit(solution)/shard_map/ppermute | solution.py:20
  22.0 15.1 %collective-permute-start.2 = (bf16[1600,128]{1,0:T(8,128)(2,1)S(1)}, bf16[1600,128]{1,0:T(8,128)(2,1)}, u32[]{:S(2)}, u32[]{:S(2)}) collective-permute-start(bf16[1600,128]{1,0:T(8,128)(2,1)S(1)} %copy-done.1), channel_id=1, source_target_pairs={{128,0},{192,64},{0,128},{64,192},{129,1},{193,65},{1,129},{65,193... | collective-permute-start | bytes 1228808 | tf_op jit(solution)/shard_map/ppermute | solution.py:20
  22.6 17.5 %collective-permute-start.3 = (bf16[1600,128]{1,0:T(8,128)(2,1)S(1)}, bf16[1600,128]{1,0:T(8,128)(2,1)}, u32[]{:S(2)}, u32[]{:S(2)}) collective-permute-start(bf16[1600,128]{1,0:T(8,128)(2,1)S(1)} %copy-done.1), channel_id=1, source_target_pairs={{192,0},{0,64},{64,128},{128,192},{193,1},{1,65},{65,129},{129,193... | collective-permute-start | bytes 1228808 | tf_op jit(solution)/shard_map/ppermute | solution.py:20
  36.3 0.7 copy-start.2
  40.1 1.0 copy-start.3
  41.1 4.3 %copy-start.10 = (bf16[128,512]{1,0:T(8,128)(2,1)S(1)}, bf16[128,512]{1,0:T(8,128)(2,1)}, u32[]{:S(2)}) copy-start(bf16[128,512]{1,0:T(8,128)(2,1)} %param.20) | copy-start | bytes 393220
  45.3 2.3 collective-permute-start.4
  45.5 13.6 %collective-permute-start.5 = (bf16[144,512]{1,0:T(8,128)(2,1)S(1)}, bf16[144,512]{1,0:T(8,128)(2,1)S(1)}, u32[]{:S(2)}, u32[]{:S(2)}) collective-permute-start(bf16[144,512]{1,0:T(8,128)(2,1)S(1)} %fusion.37.w0), channel_id=1, source_target_pairs={{64,0},{128,64},{192,128},{0,192},{65,1},{129,65},{193,129},{1,193... | collective-permute-start | bytes 442376 | tf_op jit(solution)/shard_map/ppermute | solution.py:20
  46.2 12.9 %collective-permute-start.7 = (bf16[144,512]{1,0:T(8,128)(2,1)S(1)}, bf16[144,512]{1,0:T(8,128)(2,1)S(1)}, u32[]{:S(2)}, u32[]{:S(2)}) collective-permute-start(bf16[144,512]{1,0:T(8,128)(2,1)S(1)} %fusion.37.w0), channel_id=1, source_target_pairs={{192,0},{0,64},{64,128},{128,192},{193,1},{1,65},{65,129},{129,193... | collective-permute-start | bytes 442376 | tf_op jit(solution)/shard_map/ppermute | solution.py:20
  52.0 13.3 %all-to-all-start.1 = ((bf16[4,80,384]{2,1,0:T(8,128)(2,1)}), bf16[4,80,384]{2,1,0:T(8,128)(2,1)S(1)}, u32[]{:S(2)}, u32[]{:S(2)}) async-start(bf16[4,80,384]{2,1,0:T(8,128)(2,1)} %pad_maximum_fusion.3), calls=%async_computation.1 | async-start | bytes 491520 | tf_op jit(solution)/shard_map/all_to_all | solution.py:263
  58.4 24.5 %copy-start.11 = (bf16[32,512]{1,0:T(8,128)(2,1)S(1)}, bf16[32,512]{1,0:T(8,128)(2,1)}, u32[]{:S(2)}) copy-start(bf16[32,512]{1,0:T(8,128)(2,1)} %param.22) | copy-start | bytes 98308
  58.4 6.6 %collective-permute-start.6 = (bf16[144,512]{1,0:T(8,128)(2,1)S(1)}, bf16[144,512]{1,0:T(8,128)(2,1)S(1)}, u32[]{:S(2)}, u32[]{:S(2)}) collective-permute-start(bf16[144,512]{1,0:T(8,128)(2,1)S(1)} %fusion.37.w0), channel_id=1, source_target_pairs={{128,0},{192,64},{0,128},{64,192},{129,1},{193,65},{1,129},{65,193... | collective-permute-start | bytes 442376 | tf_op jit(solution)/shard_map/ppermute | solution.py:20
  65.3 29.9 %copy-start.12 = (bf16[32,512]{1,0:T(8,128)(2,1)S(1)}, bf16[32,512]{1,0:T(8,128)(2,1)}, u32[]{:S(2)}) copy-start(bf16[32,512]{1,0:T(8,128)(2,1)} %param.23) | copy-start | bytes 98308
  65.3 30.7 %copy-start.18 = (s32[16]{0:T(128)S(1)}, s32[16]{0:T(128)}, u32[]{:S(2)}) copy-start(s32[16]{0:T(128)} %param.27) | copy-start | bytes 196
  65.4 33.7 %copy-start.17 = (f32[512]{0:T(512)S(1)}, f32[512]{0:T(512)}, u32[]{:S(2)}) copy-start(f32[512]{0:T(512)} %param.21) | copy-start | bytes 6148
  76.0 1.3 collective-permute-start.8
  78.4 11.5 %all-to-all-start.3 = ((bf16[4,64,512]{2,1,0:T(8,128)(2,1)}), bf16[4,64,512]{2,1,0:T(8,128)(2,1)S(1)}, u32[]{:S(2)}, u32[]{:S(2)}) async-start(bf16[4,64,512]{2,1,0:T(8,128)(2,1)} %bitcast.9), calls=%async_computation.3 | async-start | bytes 524288 | tf_op jit(solution)/shard_map/all_to_all | solution.py:282
  90.0 14.0 %copy-start.15 = (s32[16]{0:T(128)S(1)}, s32[16]{0:T(128)}, u32[]{:S(2)}) copy-start(s32[16]{0:T(128)} %param.29) | copy-start | bytes 196
  90.0 14.0 %copy-start.16 = (s32[16]{0:T(128)S(1)}, s32[16]{0:T(128)}, u32[]{:S(2)}) copy-start(s32[16]{0:T(128)} %param.28) | copy-start | bytes 196
  90.0 9.1 %collective-permute-start.9 = (bf16[64,512]{1,0:T(8,128)(2,1)S(1)}, bf16[64,512]{1,0:T(8,128)(2,1)S(1)}, u32[]{:S(2)}, u32[]{:S(2)}) collective-permute-start(bf16[64,512]{1,0:T(8,128)(2,1)S(1)} %convert_element_type.113), channel_id=1, source_target_pairs={{0,4},{4,0},{1,5},{5,1},{2,6},{6,2},{3,7},{7,3},{8,12},{12,8},{9,1... | collective-permute-start | bytes 196616 | tf_op jit(solution)/shard_map/ppermute | solution.py:24
  95.2 9.0 %collective-permute-start.10 = (bf16[32,1024]{1,0:T(8,128)(2,1)S(1)}, bf16[32,1024]{1,0:T(8,128)(2,1)S(1)}, u32[]{:S(2)}, u32[]{:S(2)}) collective-permute-start(bf16[32,1024]{1,0:T(8,128)(2,1)S(1)} %constant_dynamic-update-slice_fusion), channel_id=1, source_target_pairs={{0,4},{4,0},{1,5},{5,1},{2,6},{6,2},{3,7},{7,3},{8,12},{12,8},{9,1... | collective-permute-start | bytes 196616 | tf_op jit(solution)/shard_map/ppermute | solution.py:24
  100.2 23.0 %all-to-all-start.4 = ((bf16[16,64,512]{2,1,0:T(8,128)(2,1)}), bf16[16,64,512]{2,1,0:T(8,128)(2,1)S(1)}, u32[]{:S(2)}, u32[]{:S(2)}) async-start(bf16[16,64,512]{2,1,0:T(8,128)(2,1)} %broadcast_in_dim.20), calls=%async_computation.4 | async-start | bytes 2097152 | tf_op jit(solution)/shard_map/all_to_all | solution.py:29
  104.3 16.4 %collective-permute-start.13 = (bf16[64,1024]{1,0:T(8,128)(2,1)S(1)}, bf16[64,1024]{1,0:T(8,128)(2,1)S(1)}, u32[]{:S(2)}, u32[]{:S(2)}) collective-permute-start(bf16[64,1024]{1,0:T(8,128)(2,1)S(1)} %maximum_select_fusion.1), channel_id=1, source_target_pairs={{3,0},{0,1},{1,2},{2,3},{7,4},{4,5},{5,6},{6,7},{11,8},{8,9},{9,10... | collective-permute-start | bytes 393224 | tf_op jit(solution)/shard_map/ppermute | solution.py:20
  106.5 16.0 %collective-permute-start.12 = (bf16[64,1024]{1,0:T(8,128)(2,1)S(1)}, bf16[64,1024]{1,0:T(8,128)(2,1)S(1)}, u32[]{:S(2)}, u32[]{:S(2)}) collective-permute-start(bf16[64,1024]{1,0:T(8,128)(2,1)S(1)} %maximum_select_fusion.1), channel_id=1, source_target_pairs={{2,0},{3,1},{0,2},{1,3},{6,4},{7,5},{4,6},{5,7},{10,8},{11,9},{8,1... | collective-permute-start | bytes 393224 | tf_op jit(solution)/shard_map/ppermute | solution.py:20
  109.1 13.3 %collective-permute-start.11 = (bf16[64,1024]{1,0:T(8,128)(2,1)S(1)}, bf16[64,1024]{1,0:T(8,128)(2,1)S(1)}, u32[]{:S(2)}, u32[]{:S(2)}) collective-permute-start(bf16[64,1024]{1,0:T(8,128)(2,1)S(1)} %maximum_select_fusion.1), channel_id=1, source_target_pairs={{1,0},{2,1},{3,2},{0,3},{5,4},{6,5},{7,6},{4,7},{9,8},{10,9},{11,1... | collective-permute-start | bytes 393224 | tf_op jit(solution)/shard_map/ppermute | solution.py:20
  124.7 1.5 copy-start.4
  126.2 1.2 copy-start.6
  127.5 1.8 copy-start.8
  129.3 9.0 %collective-permute-start.18 = (f32[128,3584]{1,0:T(8,128)}, f32[128,3584]{1,0:T(8,128)}, u32[]{:S(2)}, u32[]{:S(2)}) collective-permute-start(f32[128,3584]{1,0:T(8,128)} %pad_maximum_fusion), channel_id=1, source_target_pairs={{0,8},{8,0},{1,9},{9,1},{2,10},{10,2},{3,11},{11,3},{4,12},{12,4},... | collective-permute-start | bytes 5505032 | tf_op jit(solution)/shard_map/ppermute | solution.py:24
  132.9 5.4 %copy-start.9 = (f32[256,1792]{1,0:T(8,128)S(1)}, f32[256,1792]{1,0:T(8,128)}, u32[]{:S(2)}) copy-start(f32[256,1792]{1,0:T(8,128)} %copy-done.8) | copy-start | bytes 5505028
  134.3 4.0 %copy-start.7 = (f32[256,1792]{1,0:T(8,128)S(1)}, f32[256,1792]{1,0:T(8,128)}, u32[]{:S(2)}) copy-start(f32[256,1792]{1,0:T(8,128)} %copy-done.6) | copy-start | bytes 5505028
  134.3 2.7 %collective-permute-start.14 = (f32[128,1792]{1,0:T(8,128)S(1)}, f32[128,1792]{1,0:T(8,128)S(1)}, u32[]{:S(2)}, u32[]{:S(2)}) collective-permute-start(f32[128,1792]{1,0:T(8,128)S(1)} %slice.197), channel_id=1, source_target_pairs={{0,8},{8,0},{1,9},{9,1},{2,10},{10,2},{3,11},{11,3},{4,12},{12,4},... | collective-permute-start | bytes 2752520 | tf_op jit(solution)/shard_map/ppermute | solution.py:24
  140.2 8.6 %collective-permute-start.21 = (bf16[32,3584]{1,0:T(8,128)(2,1)S(1)}, bf16[32,3584]{1,0:T(8,128)(2,1)S(1)}, u32[]{:S(2)}, u32[]{:S(2)}) collective-permute-start(bf16[32,3584]{1,0:T(8,128)(2,1)S(1)} %get-tuple-element.30), channel_id=1, source_target_pairs={{48,0},{0,16},{16,32},{32,48},{49,1},{1,17},{17,33},{33,49},{50,2}... | collective-permute-start | bytes 688136 | tf_op jit(solution)/shard_map/ppermute | solution.py:20
  140.2 25.6 %collective-permute-start.20 = (bf16[32,3584]{1,0:T(8,128)(2,1)S(1)}, bf16[32,3584]{1,0:T(8,128)(2,1)S(1)}, u32[]{:S(2)}, u32[]{:S(2)}) collective-permute-start(bf16[32,3584]{1,0:T(8,128)(2,1)S(1)} %get-tuple-element.31), channel_id=1, source_target_pairs={{32,0},{48,16},{0,32},{16,48},{33,1},{49,17},{1,33},{17,49},{34,2}... | collective-permute-start | bytes 688136 | tf_op jit(solution)/shard_map/ppermute | solution.py:20
  142.6 25.7 %collective-permute-start.19 = (bf16[32,3584]{1,0:T(8,128)(2,1)S(1)}, bf16[32,3584]{1,0:T(8,128)(2,1)S(1)}, u32[]{:S(2)}, u32[]{:S(2)}) collective-permute-start(bf16[32,3584]{1,0:T(8,128)(2,1)S(1)} %get-tuple-element.29), channel_id=1, source_target_pairs={{16,0},{32,16},{48,32},{0,48},{17,1},{33,17},{49,33},{1,49},{18,2}... | collective-permute-start | bytes 688136 | tf_op jit(solution)/shard_map/ppermute | solution.py:20
  142.6 25.8 %collective-permute-start.17 = (bf16[32,1792]{1,0:T(8,128)(2,1)S(1)}, bf16[32,1792]{1,0:T(8,128)(2,1)S(1)}, u32[]{:S(2)}, u32[]{:S(2)}) collective-permute-start(bf16[32,1792]{1,0:T(8,128)(2,1)S(1)} %get-tuple-element.39), channel_id=1, source_target_pairs={{48,0},{0,16},{16,32},{32,48},{49,1},{1,17},{17,33},{33,49},{50,2}... | collective-permute-start | bytes 344072 | tf_op jit(solution)/shard_map/ppermute | solution.py:20
  144.7 25.8 %collective-permute-start.16 = (bf16[32,1792]{1,0:T(8,128)(2,1)S(1)}, bf16[32,1792]{1,0:T(8,128)(2,1)S(1)}, u32[]{:S(2)}, u32[]{:S(2)}) collective-permute-start(bf16[32,1792]{1,0:T(8,128)(2,1)S(1)} %get-tuple-element.40), channel_id=1, source_target_pairs={{32,0},{48,16},{0,32},{16,48},{33,1},{49,17},{1,33},{17,49},{34,2}... | collective-permute-start | bytes 344072 | tf_op jit(solution)/shard_map/ppermute | solution.py:20
  148.7 24.4 %collective-permute-start.15 = (bf16[32,1792]{1,0:T(8,128)(2,1)S(1)}, bf16[32,1792]{1,0:T(8,128)(2,1)S(1)}, u32[]{:S(2)}, u32[]{:S(2)}) collective-permute-start(bf16[32,1792]{1,0:T(8,128)(2,1)S(1)} %get-tuple-element.38), channel_id=1, source_target_pairs={{16,0},{32,16},{48,32},{0,48},{17,1},{33,17},{49,33},{1,49},{18,2}... | collective-permute-start | bytes 344072 | tf_op jit(solution)/shard_map/ppermute | solution.py:20
  173.3 8.6 %collective-permute-start.24 = (bf16[32,3584]{1,0:T(8,128)(2,1)S(1)}, bf16[32,3584]{1,0:T(8,128)(2,1)S(1)}, u32[]{:S(2)}, u32[]{:S(2)}) collective-permute-start(bf16[32,3584]{1,0:T(8,128)(2,1)S(1)} %pad_maximum_fusion.4), channel_id=1, source_target_pairs={{48,0},{0,16},{16,32},{32,48},{49,1},{1,17},{17,33},{33,49},{50,2}... | collective-permute-start | bytes 688136 | tf_op jit(solution)/shard_map/ppermute | solution.py:20
  173.4 20.1 %collective-permute-start.23 = (bf16[32,3584]{1,0:T(8,128)(2,1)S(1)}, bf16[32,3584]{1,0:T(8,128)(2,1)S(1)}, u32[]{:S(2)}, u32[]{:S(2)}) collective-permute-start(bf16[32,3584]{1,0:T(8,128)(2,1)S(1)} %pad_maximum_fusion.4), channel_id=1, source_target_pairs={{32,0},{48,16},{0,32},{16,48},{33,1},{49,17},{1,33},{17,49},{34,2}... | collective-permute-start | bytes 688136 | tf_op jit(solution)/shard_map/ppermute | solution.py:20
  174.8 20.2 %collective-permute-start.22 = (bf16[32,3584]{1,0:T(8,128)(2,1)S(1)}, bf16[32,3584]{1,0:T(8,128)(2,1)S(1)}, u32[]{:S(2)}, u32[]{:S(2)}) collective-permute-start(bf16[32,3584]{1,0:T(8,128)(2,1)S(1)} %pad_maximum_fusion.4), channel_id=1, source_target_pairs={{16,0},{32,16},{48,32},{0,48},{17,1},{33,17},{49,33},{1,49},{18,2}... | collective-permute-start | bytes 688136 | tf_op jit(solution)/shard_map/ppermute | solution.py:20
  176.2 20.1 %copy-start.5 = (bf16[512,1792]{1,0:T(8,128)(2,1)S(1)}, bf16[512,1792]{1,0:T(8,128)(2,1)}, u32[]{:S(2)}) copy-start(bf16[512,1792]{1,0:T(8,128)(2,1)} %param.24) | copy-start | bytes 5505028
  195.1 2.8 %collective-permute-start.25 = (bf16[128,3584]{1,0:T(8,128)(2,1)S(1)}, bf16[128,3584]{1,0:T(8,128)(2,1)S(1)}, u32[]{:S(2)}, u32[]{:S(2)}) collective-permute-start(bf16[128,3584]{1,0:T(8,128)(2,1)S(1)} %pad_maximum_fusion.1), channel_id=1, source_target_pairs={{0,8},{8,0},{1,9},{9,1},{2,10},{10,2},{3,11},{11,3},{4,12},{12,4},... | collective-permute-start | bytes 2752520 | tf_op jit(solution)/shard_map/ppermute | solution.py:24
  200.3 10.6 %all-to-all-start.5 = ((bf16[4,64,512]{2,1,0:T(8,128)(2,1)}), bf16[4,64,512]{2,1,0:T(8,128)(2,1)S(1)}, u32[]{:S(2)}, u32[]{:S(2)}) async-start(bf16[4,64,512]{2,1,0:T(8,128)(2,1)} %bitcast.12), calls=%async_computation.5 | async-start | bytes 524288 | tf_op jit(solution)/shard_map/all_to_all | solution.py:326
  210.9 8.3 %collective-permute-start.26 = (bf16[64,512]{1,0:T(8,128)(2,1)S(1)}, bf16[64,512]{1,0:T(8,128)(2,1)S(1)}, u32[]{:S(2)}, u32[]{:S(2)}) collective-permute-start(bf16[64,512]{1,0:T(8,128)(2,1)S(1)} %convert_element_type.128), channel_id=1, source_target_pairs={{0,4},{4,0},{1,5},{5,1},{2,6},{6,2},{3,7},{7,3},{8,12},{12,8},{9,1... | collective-permute-start | bytes 196616 | tf_op jit(solution)/shard_map/ppermute | solution.py:24
  219.9 11.0 %all-to-all-start.6 = ((bf16[4,64,512]{2,1,0:T(8,128)(2,1)}), bf16[4,64,512]{2,1,0:T(8,128)(2,1)S(1)}, u32[]{:S(2)}, u32[]{:S(2)}) async-start(bf16[4,64,512]{2,1,0:T(8,128)(2,1)} %broadcast_in_dim.22), calls=%async_computation.6 | async-start | bytes 524288 | tf_op jit(solution)/shard_map/all_to_all | solution.py:29
  231.8 9.3 %all-to-all-start.7 = ((bf16[4,32,512]{2,1,0:T(8,128)(2,1)}), bf16[4,32,512]{2,1,0:T(8,128)(2,1)S(1)}, u32[]{:S(2)}, u32[]{:S(2)}) async-start(bf16[4,32,512]{2,1,0:T(8,128)(2,1)} %bitcast.14), calls=%async_computation.7 | async-start | bytes 262144 | tf_op jit(solution)/shard_map/all_to_all | solution.py:339
where the time goes:
time: 243 us; the launch traced here: 242 us
  waiting for transfers between devices  117 us (48%)
  starting transfers between devices  74.3 us (31%)
  other arithmetic  12.2 us (5%)
  matrix products  11.1 us (5%)
  local copies, waits for them, and re-layouts  10.3 us (4%)
  blocking collectives  9.89 us (4%)
  Pallas kernels  5.29 us (2%)
    ppermute x18, waiting for transfers between devices, from_next(): return lax.ppermute(value, axis, [((i + k) % n, i) for i in range(n)])  76.2 us
    ppermute x18, starting transfers between devices, from_next(): return lax.ppermute(value, axis, [((i + k) % n, i) for i in range(n)])  25.5 us
    ppermute x9, starting transfers between devices, swap(): return lax.ppermute(value, axis, [(0, 1), (1, 0)])  18.7 us
    ppermute x9, waiting for transfers between devices, swap(): return lax.ppermute(value, axis, [(0, 1), (1, 0)])  15.5 us
    all_to_all x3, starting transfers between devices, copy_for_each(): lax.all_to_all(jnp.broadcast_to(shard[None], (count, *shard.shape)), axis...  12.5 us
    all_to_all x1, blocking collectives, copy_for_each(): lax.all_to_all(jnp.broadcast_to(shard[None], (count, *shard.shape)), axis...  9.89 us
    all_to_all x1, waiting for transfers between devices, local(): lax.all_to_all(ordered.reshape(4, count // 4, cols), 'x', 0, 0, tiled=True)  7.18 us
    all_to_all x1, waiting for transfers between devices, local(): lax.all_to_all(second.reshape(4, count // 4, cols), 'x', 0, 0, tiled=True)  6.97 us
  transfers between devices with their start and end apart: 34, of which 24 were waited for; matrix products, arithmetic and copies ran while one was open for 7% of the time, Pallas kernels for 0%

commit v1 on v0

--- a/solution.py
+++ b/solution.py
@@ -67,8 +67,11 @@
         & (offsets[None, :] <= pos[:, None])
         & (pos[:, None] < (offsets + counts)[None, :])
     )
-    source = jnp.sum(jnp.where(hit, starts[None, :] + pos[:, None] - offsets[None, :], 0), axis=1)
-    return (source, jnp.any(hit, axis=1))
+    covered = jnp.any(hit, axis=1)
+    source = lax.optimization_barrier(
+        jnp.sum(jnp.where(hit, starts[None, :] + pos[:, None] - offsets[None, :], 0), axis=1)
+    )
+    return (source, covered)
 
 
 def image_targets(counts, sequence, offsets, rows):
@@ -96,9 +99,9 @@
     return jnp.concatenate([hi, mid, v - hi - mid], axis=axis).astype(BF)
 
 
-def row_share(whole, own):
-    there = swap(whole[4 * own :], "c")
-    near = whole[: 4 * own] + there
+def row_share(kept, given, own):
+    there = swap(given, "c")
+    near = kept + there
     sent = near[own:].astype(BF)
     total = near[:own]
     for k in (1, 2, 3):
@@ -284,34 +287,44 @@
     part = part + swap(part.astype(BF), "zh").astype(F32)
     pair_projected = (part + proj_out_bias).astype(BF)
     projected = jnp.where(zh == 0, pair_projected[:own], pair_projected[own:])
-    everything = copy_for_each(pair_projected, ("g", "x")).reshape(-1, cols)
+    line_rows = jnp.concatenate(
+        [pair_projected] + [from_next(pair_projected, "x", k) for k in (1, 2, 3)], axis=0
+    )
+    far_rows = [from_next(line_rows, "g", k) for k in (1, 2, 3)]
 
     q = jnp.arange(count, dtype=jnp.int32)
     block = ((zl + (q // own) % 4) % 4) * 2 + (c + q // (4 * own)) % 2
     at = block * own + q % own
-    source, covered = seq_sources(
-        image_counts, image_sequence, image_offsets, g * count + at
-    )
+    source, covered = seq_sources(image_counts, image_sequence, image_offsets, g * count + at)
 
     def gathered_place(r):
         return (r // own) % 4 * (2 * own) + (r // (4 * own)) % 2 * own + r % own
 
     place = gathered_place(at)
-    text_place = (place - x * (2 * own)) % count
+
+    def x_turned(p):
+        return (p - x * (2 * own)) % count
+
+    text_place = x_turned(place)
     column = jnp.where(
         covered,
-        source // count * count + gathered_place(source % count),
-        everything.shape[0] + text_place,
-    )
-    choose = (column[:, None] == jnp.arange(everything.shape[0] + count)[None, :]).astype(BF)
+        (source // count - g) % 4 * count + x_turned(gathered_place(source % count)),
+        4 * count + text_place,
+    )
+    column = lax.optimization_barrier(column)
+    choose = column[:, None]
+    near_choice = jnp.concatenate([choose == q[None, :], choose == q[None, :] + 4 * count], axis=1)
+    far_choice = choose == count + jnp.arange(3 * count)[None, :]
+    near_inputs = mm(near_choice.astype(BF), jnp.concatenate([line_rows, text], axis=0))
+    far_inputs = mm(far_choice.astype(BF), jnp.concatenate(far_rows, axis=0))
+    inputs = (near_inputs + far_inputs).astype(BF)
     reorder = (text_place[:, None] == q[None, :]).astype(BF)
-    inputs = pick(choose, jnp.concatenate([everything, text], axis=0))
     back_rows = pick(reorder, cotangent)
 
-    hidden = mm_t(back_rows, down_weight)
-    hidden_grad = row_share(hidden, own)
+    hidden = [mm_t(back_rows[k : k + 4 * own], down_weight) for k in (0, 4 * own)]
+    hidden_grad = row_share(*hidden, own)
     whole = jnp.concatenate([mm(inputs, gate_weight), mm(inputs, up_weight)], axis=1)
-    total = row_share(whole, own)
+    total = row_share(whole[: 4 * own], whole[4 * own :], own)
     gate_grad, up_grad = unit_grads(total[:, :width], total[:, width:], hidden_grad)
 
     grads = jnp.concatenate([gate_grad, up_grad], axis=1)
@@ -321,23 +334,30 @@
         mm_t(h[:, :width], gate_weight) + mm_t(h[:, width:], up_weight) for h in (line, other)
     ]
     turned = jnp.concatenate(halves, axis=0).astype(BF)
+
+    def image_rows(k):
+        base = (g - k) % 4 * count
+        row = base + q // (2 * own) * own + q // own % 2 * (4 * own) + q % own
+        target, valid = image_targets(image_counts, image_sequence, image_offsets, row)
+        held = valid & (target // count == g)
+        return (held[:, None] & ((target % count)[:, None] == at[None, :])).astype(BF)
+
+    back = []
+    for k in (2, 1, 3):
+        given = pick(image_rows(k), turned)
+        back.append(from_next(given, "g", k))
     restore = (q[:, None] == place[None, :]).astype(BF)
     ordered = pick(restore, turned)
-    parts = lax.all_to_all(ordered.reshape(4, count // 4, cols), "x", 0, 0, tiled=True)
-    part = jnp.sum(parts.astype(F32), axis=0)
-    pair_grads = (part + swap(part.astype(BF), "zh").astype(F32)).astype(BF)
-    sequence_grads = jnp.where(zh == 0, pair_grads[:own], pair_grads[own:])
-
-    column_rows = copy_for_each(pair_grads, "g").reshape(-1, cols)
-    r = jnp.arange(4 * own, dtype=jnp.int32)
-    target, valid = image_targets(
-        image_counts, image_sequence, image_offsets, g * count + zh * (4 * own) + r
-    )
-    held = valid & ((target // own) % 4 == x)
-    spot = target // count * (2 * own) + (target // (4 * own)) % 2 * own + target % own
-    give = (held[:, None] & (spot[:, None] == q[None, :])).astype(BF)
-    parts = lax.all_to_all(pick(give, column_rows).reshape(4, own, cols), "x", 0, 0, tiled=True)
-    row_grads = jnp.sum(parts.astype(F32), axis=0).astype(BF)
+    image = mm(image_rows(0), turned) + sum(b.astype(F32) for b in back)
+    both = jnp.concatenate(
+        [ordered.reshape(4, 2 * own, cols), image.astype(BF).reshape(4, 2 * own, cols)], axis=1
+    )
+    parts = lax.all_to_all(both, "x", 0, 0, tiled=True)
+    part = jnp.sum(parts.astype(F32), axis=0).reshape(2, 2, own, cols)
+    keep = jnp.where(zh == 0, part[:, 0], part[:, 1])
+    give = jnp.where(zh == 0, part[:, 1], part[:, 0]).astype(BF)
+    final = (keep + swap(give, "zh").astype(F32)).astype(BF)
+    sequence_grads, row_grads = final[0], final[1]
     return (projected, sequence_grads, row_grads)
 
 

time: 243 us -> 231 us (0.951)
  waiting for transfers between devices: 117 us -> 98.5 us
  local copies, waits for them, and re-layouts: 10.3 us -> 13.8 us
  matrix products: 11.1 us -> 7.93 us
  other arithmetic: 12.2 us -> 15.3 us
  blocking collectives: 9.89 us -> 12.5 us
    ppermute x18 -> x27, starting transfers between devices: 25.5 us -> 38.1 us  [from_next(): return lax.ppermute(value, axis, [((i + k) % n, i) for i in range(n)])]
    all_to_all x2 -> x0, waiting for transfers between devices: 12.5 us -> none  [the longest x1 7.18 us: local(): lax.all_to_all(ordered.reshape(4, count // 4, cols), 'x', 0, 0, tiled=True)]
    ppermute x18 -> x27, waiting for transfers between devices: 76.2 us -> 63.9 us  [from_next(): return lax.ppermute(value, axis, [((i + k) % n, i) for i in range(n)])]
    all_to_all x2 -> x0, starting transfers between devices: 6.73 us -> none  [the longest x1 3.4 us: local(): lax.all_to_all(ordered.reshape(4, count // 4, cols), 'x', 0, 0, tiled=True)]
    all_to_all x1, waiting for transfers between devices: 0.18 us -> 6.83 us  [local(): parts = lax.all_to_all(message, 'zl', 0, 0, tiled=True).astype(F32)]
    all_to_all x3 -> x2, starting transfers between devices: 12.5 us -> 9.46 us  [copy_for_each(): lax.all_to_all(jnp.broadcast_to(shard[None], (count, *shard.shape)), axis...]
    all_to_all x1, starting transfers between devices: 6.43 us -> 3.79 us  [local(): parts = lax.all_to_all(message, 'zl', 0, 0, tiled=True).astype(F32)]
    all_to_all x1, blocking collectives: 9.89 us -> 12.5 us  [local(): parts = lax.all_to_all(both, 'x', 0, 0, tiled=True)]
  transfers between devices with their start and end apart: 34 -> 40, of which waited for: 24 -> 26; matrix products, arithmetic and copies ran while one was open for 7% -> 12% of each run, Pallas kernels for 0% -> 3%
where the time goes in v1:
time: 231 us; the launch traced here: 230 us
  waiting for transfers between devices  98.5 us (43%)
  starting transfers between devices  74.3 us (32%)
  other arithmetic  15.3 us (7%)
  local copies, waits for them, and re-layouts  13.8 us (6%)
  blocking collectives  12.5 us (5%)
  matrix products  7.93 us (3%)
  Pallas kernels  6.18 us (3%)
    ppermute x27, waiting for transfers between devices, from_next(): return lax.ppermute(value, axis, [((i + k) % n, i) for i in range(n)])  63.9 us
    ppermute x27, starting transfers between devices, from_next(): return lax.ppermute(value, axis, [((i + k) % n, i) for i in range(n)])  38.1 us
    ppermute x9, starting transfers between devices, swap(): return lax.ppermute(value, axis, [(0, 1), (1, 0)])  18.2 us
    ppermute x9, waiting for transfers between devices, swap(): return lax.ppermute(value, axis, [(0, 1), (1, 0)])  15.8 us
    all_to_all x1, blocking collectives, local(): parts = lax.all_to_all(both, 'x', 0, 0, tiled=True)  12.5 us
    all_to_all x2, starting transfers between devices, copy_for_each(): lax.all_to_all(jnp.broadcast_to(shard[None], (count, *shard.shape)), axis...  9.46 us
    all_to_all x1, waiting for transfers between devices, local(): lax.all_to_all(second.reshape(4, count // 4, cols), 'x', 0, 0, tiled=True)  6.83 us
    all_to_all x1, waiting for transfers between devices, local(): parts = lax.all_to_all(message, 'zl', 0, 0, tiled=True).astype(F32)  6.83 us
  transfers between devices with their start and end apart: 40, of which 26 were waited for; matrix products, arithmetic and copies ran while one was open for 12% of the time, Pallas kernels for 3%

profile of v1, /device:TPU:32, one launch (start us, length us, event | category | flops | bytes accessed | tf_op | source)
XLA Modules:
  0.0 229.8 jit_solution(249884137267526741)
XLA Ops:
  0.7 3.1 %collective-permute-start.1 = (bf16[1600,128]{1,0:T(8,128)(2,1)}, bf16[1600,128]{1,0:T(8,128)(2,1)S(1)}, u32[]{:S(2)}, u32[]{:S(2)}) collective-permute-start(bf16[1600,128]{1,0:T(8,128)(2,1)} %w0.1), channel_id=1, source_target_pairs={{64,0},{128,64},{192,128},{0,192},{65,1},{129,65},{193,129},{1,193... | collective-permute-start | bytes 1228808 | tf_op jit(solution)/shard_map/ppermute | solution.py:20
  4.4 1.0 collective-permute-start.3
  5.3 6.3 %collective-permute-start = (bf16[32,1600]{1,0:T(8,128)(2,1)}, bf16[32,1600]{1,0:T(8,128)(2,1)S(1)}, u32[]{:S(2)}, u32[]{:S(2)}) collective-permute-start(bf16[32,1600]{1,0:T(8,128)(2,1)} %param.15), channel_id=1, source_target_pairs={{0,4},{4,0},{1,5},{5,1},{2,6},{6,2},{3,7},{7,3},{8,12},{12,8},{9,1... | collective-permute-start | bytes 307208 | tf_op jit(solution)/shard_map/ppermute | solution.py:24
  12.8 2.9 %collective-permute-done = bf16[32,1600]{1,0:T(8,128)(2,1)S(1)} collective-permute-done((bf16[32,1600]{1,0:T(8,128)(2,1)}, bf16[32,1600]{1,0:T(8,128)(2,1)S(1)}, u32[]{:S(2)}, u32[]{:S(2)}) %collective-permute-start) | collective-permute-done | bytes 102432 | tf_op jit(solution)/shard_map/ppermute | solution.py:24
  15.8 1.0 maximum_select_fusion
  16.8 1.0 broadcast_in_dim.13
  17.8 4.3 %all-to-all-start = ((bf16[4,64,1600]{2,1,0:T(8,128)(2,1)}), bf16[4,64,1600]{2,1,0:T(8,128)(2,1)S(1)}, u32[]{:S(2)}, u32[]{:S(2)}) async-start(bf16[4,64,1600]{2,1,0:T(8,128)(2,1)} %broadcast_in_dim.13), calls=%async_computation | async-start | bytes 1703936 | tf_op jit(solution)/shard_map/all_to_all | solution.py:29
  22.1 2.3 %collective-permute-start.5 = (bf16[144,512]{1,0:T(8,128)(2,1)S(1)}, bf16[144,512]{1,0:T(8,128)(2,1)S(1)}, u32[]{:S(2)}, u32[]{:S(2)}) collective-permute-start(bf16[144,512]{1,0:T(8,128)(2,1)S(1)} %fusion.48.w0), channel_id=1, source_target_pairs={{64,0},{128,64},{192,128},{0,192},{65,1},{129,65},{193,129},{1,193... | collective-permute-start | bytes 442376 | tf_op jit(solution)/shard_map/ppermute | solution.py:20
  24.4 1.3 reshape.821.bias_ref
  25.7 1.3 copy.41
  30.2 1.4 constant_dynamic-update-slice_fusion.1
  31.6 1.4 constant_dynamic-update-slice_fusion
  33.7 2.1 collective-permute-start.6
  35.8 6.3 %collective-permute-start.10 = (bf16[32,1024]{1,0:T(8,128)(2,1)}, bf16[32,1024]{1,0:T(8,128)(2,1)}, u32[]{:S(2)}, u32[]{:S(2)}) collective-permute-start(bf16[32,1024]{1,0:T(8,128)(2,1)} %constant_dynamic-update-slice_fusion), channel_id=1, source_target_pairs={{0,4},{4,0},{1,5},{5,1},{2,6},{6,2},{3,7},{7,3},{8,12},{12,8},{9,1... | collective-permute-start | bytes 196616 | tf_op jit(solution)/shard_map/ppermute | solution.py:24
  42.1 1.0 copy-done.1
  43.1 1.0 copy-done.3
  44.8 4.2 %first_layer.1 = (f32[272,384]{1,0:T(8,128)S(1)}, f32[272,384]{1,0:T(8,128)S(1)}) custom-call(s32[1]{0:T(128)} %bitcast.c_ref, bf16[256,1600]{1,0:T(8,128)(2,1)S(1)} %bitcast.56, f32[1,1600]{1,0:T(1,128)S(1)} %reshape.820.gain_ref, f32[1,1600]{1,0:T(1,128)S(1)} %copy-done.4, bf16[1600,128]{1,0:T(8,128)(2,1)S(1)} %copy-done.1, ...), custom_call_target="tpu_custom_call" | custom-call | flops 419430400 | bytes 4194304 | tf_op jit(solution)/shard_map/first_layer/pallas_call | solution.py:160
  49.8 1.3 fusion.127
  52.9 1.7 concatenate.89
  54.7 0.9 fusion.47
  56.3 3.8 %all-to-all-start.1 = ((bf16[4,80,384]{2,1,0:T(8,128)(2,1)}), bf16[4,80,384]{2,1,0:T(8,128)(2,1)S(1)}, u32[]{:S(2)}, u32[]{:S(2)}) async-start(bf16[4,80,384]{2,1,0:T(8,128)(2,1)} %pad_maximum_fusion.6), calls=%async_computation.1 | async-start | bytes 491520 | tf_op jit(solution)/shard_map/all_to_all | solution.py:266
  60.8 6.8 %all-to-all-done.1 = bf16[4,80,384]{2,1,0:T(8,128)(2,1)S(1)} async-done(((bf16[4,80,384]{2,1,0:T(8,128)(2,1)}), bf16[4,80,384]{2,1,0:T(8,128)(2,1)S(1)}, u32[]{:S(2)}, u32[]{:S(2)}) %all-to-all-start.1) | async-done | bytes 245792 | tf_op jit(solution)/shard_map/all_to_all | solution.py:266
  69.1 5.2 %all-to-all-start.2 = ((bf16[4,64,256]{2,1,0:T(8,128)(2,1)}), bf16[4,64,256]{2,1,0:T(8,128)(2,1)S(1)}, u32[]{:S(2)}, u32[]{:S(2)}) async-start(bf16[4,64,256]{2,1,0:T(8,128)(2,1)} %broadcast_in_dim.15), calls=%async_computation.2 | async-start | bytes 262144 | tf_op jit(solution)/shard_map/all_to_all | solution.py:29
  74.3 5.1 %all-to-all-done.2 = bf16[4,64,256]{2,1,0:T(8,128)(2,1)S(1)} async-done(((bf16[4,64,256]{2,1,0:T(8,128)(2,1)}), bf16[4,64,256]{2,1,0:T(8,128)(2,1)S(1)}, u32[]{:S(2)}, u32[]{:S(2)}) %all-to-all-start.2) | async-done | bytes 131104 | tf_op jit(solution)/shard_map/all_to_all | solution.py:29
  79.5 1.3 collective-permute-done.8.other_ref
  80.8 2.0 second_layer.1
  82.8 4.8 %all-to-all-start.3 = ((bf16[4,64,512]{2,1,0:T(8,128)(2,1)}), bf16[4,64,512]{2,1,0:T(8,128)(2,1)S(1)}, u32[]{:S(2)}, u32[]{:S(2)}) async-start(bf16[4,64,512]{2,1,0:T(8,128)(2,1)} %bitcast.9), calls=%async_computation.3 | async-start | bytes 524288 | tf_op jit(solution)/shard_map/all_to_all | solution.py:285
  87.8 6.8 %all-to-all-done.3 = bf16[4,64,512]{2,1,0:T(8,128)(2,1)S(1)} async-done(((bf16[4,64,512]{2,1,0:T(8,128)(2,1)}), bf16[4,64,512]{2,1,0:T(8,128)(2,1)S(1)}, u32[]{:S(2)}, u32[]{:S(2)}) %all-to-all-start.3) | async-done | bytes 262176 | tf_op jit(solution)/shard_map/all_to_all | solution.py:285
  94.8 1.0 maximum_select_fusion.1
  96.6 2.1 collective-permute-start.12
  99.4 4.2 %collective-permute-done.9 = bf16[64,512]{1,0:T(8,128)(2,1)S(1)} collective-permute-done((bf16[64,512]{1,0:T(8,128)(2,1)S(1)}, bf16[64,512]{1,0:T(8,128)(2,1)S(1)}, u32[]{:S(2)}, u32[]{:S(2)}) %collective-permute-start.9) | collective-permute-done | bytes 65568 | tf_op jit(solution)/shard_map/ppermute | solution.py:24
  104.3 2.1 collective-permute-start.19
  107.1 2.1 collective-permute-done.20
  109.2 0.9 collective-permute-done.19
  110.8 2.1 collective-permute-start.23
  112.9 1.7 collective-permute-start.22
  114.6 1.1 collective-permute-start.21
  115.7 4.0 %collective-permute-done.23 = bf16[256,512]{1,0:T(8,128)(2,1)S(1)} collective-permute-done((bf16[256,512]{1,0:T(8,128)(2,1)S(1)}, bf16[256,512]{1,0:T(8,128)(2,1)S(1)}, u32[]{:S(2)}, u32[]{:S(2)}) %collective-permute-start.23) | collective-permute-done | bytes 262176 | tf_op jit(solution)/shard_map/ppermute | solution.py:20
  119.7 2.8 %collective-permute-done.22 = bf16[256,512]{1,0:T(8,128)(2,1)S(1)} collective-permute-done((bf16[256,512]{1,0:T(8,128)(2,1)S(1)}, bf16[256,512]{1,0:T(8,128)(2,1)S(1)}, u32[]{:S(2)}, u32[]{:S(2)}) %collective-permute-start.22) | collective-permute-done | bytes 262176 | tf_op jit(solution)/shard_map/ppermute | solution.py:20
  124.1 0.8 copy-done.6
  127.7 3.3 %collective-permute-done.14 = f32[128,1792]{1,0:T(8,128)S(1)} collective-permute-done((f32[128,1792]{1,0:T(8,128)S(1)}, f32[128,1792]{1,0:T(8,128)S(1)}, u32[]{:S(2)}, u32[]{:S(2)}) %collective-permute-start.14) | collective-permute-done | bytes 917536 | tf_op jit(solution)/shard_map/ppermute | solution.py:24
  132.1 3.2 %collective-permute-start.26 = (bf16[32,3584]{1,0:T(8,128)(2,1)S(1)}, bf16[32,3584]{1,0:T(8,128)(2,1)S(1)}, u32[]{:S(2)}, u32[]{:S(2)}) collective-permute-start(bf16[32,3584]{1,0:T(8,128)(2,1)S(1)} %get-tuple-element.38), channel_id=1, source_target_pairs={{32,0},{48,16},{0,32},{16,48},{33,1},{49,17},{1,33},{17,49},{34,2}... | collective-permute-start | bytes 688136 | tf_op jit(solution)/shard_map/ppermute | solution.py:20
  135.4 2.3 %collective-permute-start.17 = (bf16[32,1792]{1,0:T(8,128)(2,1)S(1)}, bf16[32,1792]{1,0:T(8,128)(2,1)S(1)}, u32[]{:S(2)}, u32[]{:S(2)}) collective-permute-start(bf16[32,1792]{1,0:T(8,128)(2,1)S(1)} %get-tuple-element.46), channel_id=1, source_target_pairs={{48,0},{0,16},{16,32},{32,48},{49,1},{1,17},{17,33},{33,49},{50,2}... | collective-permute-start | bytes 344072 | tf_op jit(solution)/shard_map/ppermute | solution.py:20
  137.7 1.8 collective-permute-start.16
  139.5 1.1 collective-permute-done.27
  140.6 2.8 %collective-permute-start.15 = (bf16[32,1792]{1,0:T(8,128)(2,1)S(1)}, bf16[32,1792]{1,0:T(8,128)(2,1)S(1)}, u32[]{:S(2)}, u32[]{:S(2)}) collective-permute-start(bf16[32,1792]{1,0:T(8,128)(2,1)S(1)} %get-tuple-element.45), channel_id=1, source_target_pairs={{16,0},{32,16},{48,32},{0,48},{17,1},{33,17},{49,33},{1,49},{18,2}... | collective-permute-start | bytes 344072 | tf_op jit(solution)/shard_map/ppermute | solution.py:20
  143.4 14.4 %collective-permute-done.26 = bf16[32,3584]{1,0:T(8,128)(2,1)S(1)} collective-permute-done((bf16[32,3584]{1,0:T(8,128)(2,1)S(1)}, bf16[32,3584]{1,0:T(8,128)(2,1)S(1)}, u32[]{:S(2)}, u32[]{:S(2)}) %collective-permute-start.26) | collective-permute-done | bytes 229408 | tf_op jit(solution)/shard_map/ppermute | solution.py:20
  157.8 3.0 %collective-permute-done.25 = bf16[32,3584]{1,0:T(8,128)(2,1)S(1)} collective-permute-done((bf16[32,3584]{1,0:T(8,128)(2,1)S(1)}, bf16[32,3584]{1,0:T(8,128)(2,1)S(1)}, u32[]{:S(2)}, u32[]{:S(2)}) %collective-permute-start.25) | collective-permute-done | bytes 229408 | tf_op jit(solution)/shard_map/ppermute | solution.py:20
  160.9 1.2 collective-permute-done.16
  162.1 3.5 %collective-permute-done.15 = bf16[32,1792]{1,0:T(8,128)(2,1)S(1)} collective-permute-done((bf16[32,1792]{1,0:T(8,128)(2,1)S(1)}, bf16[32,1792]{1,0:T(8,128)(2,1)S(1)}, u32[]{:S(2)}, u32[]{:S(2)}) %collective-permute-start.15) | collective-permute-done | bytes 114720 | tf_op jit(solution)/shard_map/ppermute | solution.py:20
  165.9 1.5 collective-permute-start.29
  167.9 6.4 %collective-permute-done.30 = bf16[32,3584]{1,0:T(8,128)(2,1)S(1)} collective-permute-done((bf16[32,3584]{1,0:T(8,128)(2,1)S(1)}, bf16[32,3584]{1,0:T(8,128)(2,1)S(1)}, u32[]{:S(2)}, u32[]{:S(2)}) %collective-permute-start.30) | collective-permute-done | bytes 229408 | tf_op jit(solution)/shard_map/ppermute | solution.py:20
  174.3 11.6 %collective-permute-done.29 = bf16[32,3584]{1,0:T(8,128)(2,1)S(1)} collective-permute-done((bf16[32,3584]{1,0:T(8,128)(2,1)S(1)}, bf16[32,3584]{1,0:T(8,128)(2,1)S(1)}, u32[]{:S(2)}, u32[]{:S(2)}) %collective-permute-start.29) | collective-permute-done | bytes 229408 | tf_op jit(solution)/shard_map/ppermute | solution.py:20
  185.9 1.6 collective-permute-done.28
  189.1 1.0 collective-permute-done.31
  191.8 1.8 collective-permute-start.34
  193.9 1.6 collective-permute-start.33
  195.8 1.4 collective-permute-start.32
  197.4 4.1 %collective-permute-done.34 = bf16[256,512]{1,0:T(8,128)(2,1)S(1)} collective-permute-done((bf16[256,512]{1,0:T(8,128)(2,1)S(1)}, bf16[256,512]{1,0:T(8,128)(2,1)S(1)}, u32[]{:S(2)}, u32[]{:S(2)}) %collective-permute-start.34) | collective-permute-done | bytes 262176 | tf_op jit(solution)/shard_map/ppermute | solution.py:20
  201.5 1.7 collective-permute-done.33
  203.1 4.8 %collective-permute-done.32 = bf16[256,512]{1,0:T(8,128)(2,1)S(1)} collective-permute-done((bf16[256,512]{1,0:T(8,128)(2,1)S(1)}, bf16[256,512]{1,0:T(8,128)(2,1)S(1)}, u32[]{:S(2)}, u32[]{:S(2)}) %collective-permute-start.32) | collective-permute-done | bytes 262176 | tf_op jit(solution)/shard_map/ppermute | solution.py:20
  208.3 12.5 %all_to_all.25 = bf16[4,128,512]{2,1,0:T(8,128)(2,1)S(1)} all-to-all(bf16[4,128,512]{2,1,0:T(8,128)(2,1)S(1)} %pad_maximum_fusion.3), channel_id=1, replica_groups=mesh['g'=4,'zl'=4,'c'=2,'zh'=2,'x'=4] {'x'}, dimensions={0} | all-to-all | bytes 1048576 | tf_op jit(solution)/shard_map/all_to_all | solution.py:355
  220.9 4.6 %collective-permute-start.35 = (bf16[2,32,512]{2,1,0:T(8,128)(2,1)S(1)}, bf16[2,32,512]{2,1,0:T(8,128)(2,1)S(1)}, u32[]{:S(2)}, u32[]{:S(2)}) collective-permute-start(bf16[2,32,512]{2,1,0:T(8,128)(2,1)S(1)} %fusion.76), channel_id=1, source_target_pairs={{0,4},{4,0},{1,5},{5,1},{2,6},{6,2},{3,7},{7,3},{8,12},{12,8},{9,1... | collective-permute-start | bytes 196616 | tf_op jit(solution)/shard_map/ppermute | solution.py:24
  226.1 3.1 %collective-permute-done.35 = bf16[2,32,512]{2,1,0:T(8,128)(2,1)S(1)} collective-permute-done((bf16[2,32,512]{2,1,0:T(8,128)(2,1)S(1)}, bf16[2,32,512]{2,1,0:T(8,128)(2,1)S(1)}, u32[]{:S(2)}, u32[]{:S(2)}) %collective-permute-start.35) | collective-permute-done | bytes 65568 | tf_op jit(solution)/shard_map/ppermute | solution.py:24
  (166 shorter events, 28.3 us)
Async XLA Ops:
  0.6 125.5 %copy-start = (bf16[1792,512]{1,0:T(8,128)(2,1)S(1)}, bf16[1792,512]{1,0:T(8,128)(2,1)}, u32[]{:S(2)}) copy-start(bf16[1792,512]{1,0:T(8,128)(2,1)} %param.26) | copy-start | bytes 5505028
  0.6 21.4 %copy-start.7 = (bf16[128,512]{1,0:T(8,128)(2,1)S(1)}, bf16[128,512]{1,0:T(8,128)(2,1)}, u32[]{:S(2)}) copy-start(bf16[128,512]{1,0:T(8,128)(2,1)} %param.20) | copy-start | bytes 393220
  0.7 32.3 %collective-permute-start.1 = (bf16[1600,128]{1,0:T(8,128)(2,1)}, bf16[1600,128]{1,0:T(8,128)(2,1)S(1)}, u32[]{:S(2)}, u32[]{:S(2)}) collective-permute-start(bf16[1600,128]{1,0:T(8,128)(2,1)} %w0.1), channel_id=1, source_target_pairs={{64,0},{128,64},{192,128},{0,192},{65,1},{129,65},{193,129},{1,193... | collective-permute-start | bytes 1228808 | tf_op jit(solution)/shard_map/ppermute | solution.py:20
  3.7 32.1 %collective-permute-start.2 = (bf16[1600,128]{1,0:T(8,128)(2,1)}, bf16[1600,128]{1,0:T(8,128)(2,1)}, u32[]{:S(2)}, u32[]{:S(2)}) collective-permute-start(bf16[1600,128]{1,0:T(8,128)(2,1)} %w0.1), channel_id=1, source_target_pairs={{128,0},{192,64},{0,128},{64,192},{129,1},{193,65},{1,129},{65,193... | collective-permute-start | bytes 1228808 | tf_op jit(solution)/shard_map/ppermute | solution.py:20
  4.4 37.7 %collective-permute-start.3 = (bf16[1600,128]{1,0:T(8,128)(2,1)}, bf16[1600,128]{1,0:T(8,128)(2,1)}, u32[]{:S(2)}, u32[]{:S(2)}) collective-permute-start(bf16[1600,128]{1,0:T(8,128)(2,1)} %w0.1), channel_id=1, source_target_pairs={{192,0},{0,64},{64,128},{128,192},{193,1},{1,65},{65,129},{129,193... | collective-permute-start | bytes 1228808 | tf_op jit(solution)/shard_map/ppermute | solution.py:20
  5.3 10.4 %collective-permute-start = (bf16[32,1600]{1,0:T(8,128)(2,1)}, bf16[32,1600]{1,0:T(8,128)(2,1)S(1)}, u32[]{:S(2)}, u32[]{:S(2)}) collective-permute-start(bf16[32,1600]{1,0:T(8,128)(2,1)} %param.15), channel_id=1, source_target_pairs={{0,4},{4,0},{1,5},{5,1},{2,6},{6,2},{3,7},{7,3},{8,12},{12,8},{9,1... | collective-permute-start | bytes 307208 | tf_op jit(solution)/shard_map/ppermute | solution.py:24
  16.8 7.6 %copy-start.20 = (f32[1600]{0:T(1024)S(1)}, f32[1600]{0:T(1024)}, u32[]{:S(2)}) copy-start(f32[1600]{0:T(1024)} %param.16) | copy-start | bytes 19204
  17.8 24.3 %all-to-all-start = ((bf16[4,64,1600]{2,1,0:T(8,128)(2,1)}), bf16[4,64,1600]{2,1,0:T(8,128)(2,1)S(1)}, u32[]{:S(2)}, u32[]{:S(2)}) async-start(bf16[4,64,1600]{2,1,0:T(8,128)(2,1)} %broadcast_in_dim.13), calls=%async_computation | async-start | bytes 1703936 | tf_op jit(solution)/shard_map/all_to_all | solution.py:29
  22.1 38.0 %collective-permute-start.5 = (bf16[144,512]{1,0:T(8,128)(2,1)S(1)}, bf16[144,512]{1,0:T(8,128)(2,1)S(1)}, u32[]{:S(2)}, u32[]{:S(2)}) collective-permute-start(bf16[144,512]{1,0:T(8,128)(2,1)S(1)} %fusion.48.w0), channel_id=1, source_target_pairs={{64,0},{128,64},{192,128},{0,192},{65,1},{129,65},{193,129},{1,193... | collective-permute-start | bytes 442376 | tf_op jit(solution)/shard_map/ppermute | solution.py:20
  24.4 35.7 %collective-permute-start.7 = (bf16[144,512]{1,0:T(8,128)(2,1)S(1)}, bf16[144,512]{1,0:T(8,128)(2,1)S(1)}, u32[]{:S(2)}, u32[]{:S(2)}) collective-permute-start(bf16[144,512]{1,0:T(8,128)(2,1)S(1)} %fusion.48.w0), channel_id=1, source_target_pairs={{192,0},{0,64},{64,128},{128,192},{193,1},{1,65},{65,129},{129,193... | collective-permute-start | bytes 442376 | tf_op jit(solution)/shard_map/ppermute | solution.py:20
  33.0 0.8 copy-start.2
  33.7 26.4 %collective-permute-start.6 = (bf16[144,512]{1,0:T(8,128)(2,1)S(1)}, bf16[144,512]{1,0:T(8,128)(2,1)}, u32[]{:S(2)}, u32[]{:S(2)}) collective-permute-start(bf16[144,512]{1,0:T(8,128)(2,1)S(1)} %fusion.48.w0), channel_id=1, source_target_pairs={{128,0},{192,64},{0,128},{64,192},{129,1},{193,65},{1,129},{65,193... | collective-permute-start | bytes 442376 | tf_op jit(solution)/shard_map/ppermute | solution.py:20
  35.8 59.0 %collective-permute-start.10 = (bf16[32,1024]{1,0:T(8,128)(2,1)}, bf16[32,1024]{1,0:T(8,128)(2,1)}, u32[]{:S(2)}, u32[]{:S(2)}) collective-permute-start(bf16[32,1024]{1,0:T(8,128)(2,1)} %constant_dynamic-update-slice_fusion), channel_id=1, source_target_pairs={{0,4},{4,0},{1,5},{5,1},{2,6},{6,2},{3,7},{7,3},{8,12},{12,8},{9,1... | collective-permute-start | bytes 196616 | tf_op jit(solution)/shard_map/ppermute | solution.py:24
  42.1 7.0 %copy-start.18 = (s32[16]{0:T(128)S(1)}, s32[16]{0:T(128)}, u32[]{:S(2)}) copy-start(s32[16]{0:T(128)} %reduce.5) | copy-start | bytes 196
  42.1 9.0 %copy-start.8 = (s32[256]{0:T(256)S(1)}, s32[256]{0:T(256)}, u32[]{:S(2)}) copy-start(s32[256]{0:T(256)} %get-tuple-element.77) | copy-start | bytes 3076
  42.1 9.0 %copy-start.10 = (s32[256]{0:T(256)S(1)}, s32[256]{0:T(256)}, u32[]{:S(2)}) copy-start(s32[256]{0:T(256)} %get-tuple-element.78) | copy-start | bytes 3076
  42.1 9.0 %copy-start.12 = (s32[256]{0:T(256)S(1)}, s32[256]{0:T(256)}, u32[]{:S(2)}) copy-start(s32[256]{0:T(256)} %get-tuple-element.75) | copy-start | bytes 3076
  42.1 1.0 copy-start.1
  43.1 1.0 copy-start.3
  44.1 0.7 copy-start.4
  44.8 5.0 %copy-start.16 = (s32[256]{0:T(256)S(1)}, s32[256]{0:T(256)}, u32[]{:S(2)}) copy-start(s32[256]{0:T(256)} %get-tuple-element.70) | copy-start | bytes 3076
  44.8 5.0 %copy-start.17 = (s32[256]{0:T(256)S(1)}, s32[256]{0:T(256)}, u32[]{:S(2)}) copy-start(s32[256]{0:T(256)} %get-tuple-element.71) | copy-start | bytes 3076
  44.8 6.3 %copy-start.14 = (s32[256]{0:T(256)S(1)}, s32[256]{0:T(256)}, u32[]{:S(2)}) copy-start(s32[256]{0:T(256)} %get-tuple-element.76) | copy-start | bytes 3076
  49.0 2.9 %collective-permute-start.4 = (f32[272,384]{1,0:T(8,128)S(1)}, f32[272,384]{1,0:T(8,128)S(1)}, u32[]{:S(2)}, u32[]{:S(2)}) collective-permute-start(f32[272,384]{1,0:T(8,128)S(1)} %get-tuple-element.6), channel_id=1, source_target_pairs={{0,8},{8,0},{1,9},{9,1},{2,10},{10,2},{3,11},{11,3},{4,12},{12,4},... | collective-permute-start | bytes 1253384 | tf_op jit(solution)/shard_map/ppermute | solution.py:24
  54.6 13.6 %copy-start.22 = (f32[128]{0:T(128)S(1)}, f32[128]{0:T(128)}, u32[]{:S(2)}) copy-start(f32[128]{0:T(128)} %get-tuple-element.30) | copy-start | bytes 1540
  54.7 19.6 %copy-start.23 = (pred[256]{0:T(512)(128)(4,1)S(1)}, pred[256]{0:T(512)(128)(4,1)}, u32[]{:S(2)}) copy-start(pred[256]{0:T(512)(128)(4,1)} %fusion.127) | copy-start | bytes 772
  56.3 11.4 %all-to-all-start.1 = ((bf16[4,80,384]{2,1,0:T(8,128)(2,1)}), bf16[4,80,384]{2,1,0:T(8,128)(2,1)S(1)}, u32[]{:S(2)}, u32[]{:S(2)}) async-start(bf16[4,80,384]{2,1,0:T(8,128)(2,1)} %pad_maximum_fusion.6), calls=%async_computation.1 | async-start | bytes 491520 | tf_op jit(solution)/shard_map/all_to_all | solution.py:266
  67.7 35.9 %copy-start.21 = (f32[512]{0:T(512)S(1)}, f32[512]{0:T(512)}, u32[]{:S(2)}) copy-start(f32[512]{0:T(512)} %param.21) | copy-start | bytes 6148
  69.1 10.3 %all-to-all-start.2 = ((bf16[4,64,256]{2,1,0:T(8,128)(2,1)}), bf16[4,64,256]{2,1,0:T(8,128)(2,1)S(1)}, u32[]{:S(2)}, u32[]{:S(2)}) async-start(bf16[4,64,256]{2,1,0:T(8,128)(2,1)} %broadcast_in_dim.15), calls=%async_computation.2 | async-start | bytes 262144 | tf_op jit(solution)/shard_map/all_to_all | solution.py:29
  79.4 1.3 collective-permute-start.8
  82.8 11.8 %all-to-all-start.3 = ((bf16[4,64,512]{2,1,0:T(8,128)(2,1)}), bf16[4,64,512]{2,1,0:T(8,128)(2,1)S(1)}, u32[]{:S(2)}, u32[]{:S(2)}) async-start(bf16[4,64,512]{2,1,0:T(8,128)(2,1)} %bitcast.9), calls=%async_computation.3 | async-start | bytes 524288 | tf_op jit(solution)/shard_map/all_to_all | solution.py:285
  94.6 9.0 %collective-permute-start.9 = (bf16[64,512]{1,0:T(8,128)(2,1)S(1)}, bf16[64,512]{1,0:T(8,128)(2,1)S(1)}, u32[]{:S(2)}, u32[]{:S(2)}) collective-permute-start(bf16[64,512]{1,0:T(8,128)(2,1)S(1)} %convert_element_type.136), channel_id=1, source_target_pairs={{0,4},{4,0},{1,5},{5,1},{2,6},{6,2},{3,7},{7,3},{8,12},{12,8},{9,1... | collective-permute-start | bytes 196616 | tf_op jit(solution)/shard_map/ppermute | solution.py:24
  95.8 10.6 %collective-permute-start.13 = (bf16[64,1024]{1,0:T(8,128)(2,1)S(1)}, bf16[64,1024]{1,0:T(8,128)(2,1)S(1)}, u32[]{:S(2)}, u32[]{:S(2)}) collective-permute-start(bf16[64,1024]{1,0:T(8,128)(2,1)S(1)} %maximum_select_fusion.1), channel_id=1, source_target_pairs={{3,0},{0,1},{1,2},{2,3},{7,4},{4,5},{5,6},{6,7},{11,8},{8,9},{9,10... | collective-permute-start | bytes 393224 | tf_op jit(solution)/shard_map/ppermute | solution.py:20
  96.6 10.4 %collective-permute-start.12 = (bf16[64,1024]{1,0:T(8,128)(2,1)S(1)}, bf16[64,1024]{1,0:T(8,128)(2,1)S(1)}, u32[]{:S(2)}, u32[]{:S(2)}) collective-permute-start(bf16[64,1024]{1,0:T(8,128)(2,1)S(1)} %maximum_select_fusion.1), channel_id=1, source_target_pairs={{2,0},{3,1},{0,2},{1,3},{6,4},{7,5},{4,6},{5,7},{10,8},{11,9},{8,1... | collective-permute-start | bytes 393224 | tf_op jit(solution)/shard_map/ppermute | solution.py:20
  98.7 8.4 %collective-permute-start.11 = (bf16[64,1024]{1,0:T(8,128)(2,1)S(1)}, bf16[64,1024]{1,0:T(8,128)(2,1)S(1)}, u32[]{:S(2)}, u32[]{:S(2)}) collective-permute-start(bf16[64,1024]{1,0:T(8,128)(2,1)S(1)} %maximum_select_fusion.1), channel_id=1, source_target_pairs={{1,0},{2,1},{3,2},{0,3},{5,4},{6,5},{7,6},{4,7},{9,8},{10,9},{11,1... | collective-permute-start | bytes 393224 | tf_op jit(solution)/shard_map/ppermute | solution.py:20
  103.6 5.6 %collective-permute-start.20 = (bf16[64,512]{1,0:T(8,128)(2,1)S(1)}, bf16[64,512]{1,0:T(8,128)(2,1)S(1)}, u32[]{:S(2)}, u32[]{:S(2)}) collective-permute-start(bf16[64,512]{1,0:T(8,128)(2,1)S(1)} %get-tuple-element.27), channel_id=1, source_target_pairs={{3,0},{0,1},{1,2},{2,3},{7,4},{4,5},{5,6},{6,7},{11,8},{8,9},{9,10... | collective-permute-start | bytes 196616 | tf_op jit(solution)/shard_map/ppermute | solution.py:20
  104.3 5.8 %collective-permute-start.19 = (bf16[64,512]{1,0:T(8,128)(2,1)S(1)}, bf16[64,512]{1,0:T(8,128)(2,1)S(1)}, u32[]{:S(2)}, u32[]{:S(2)}) collective-permute-start(bf16[64,512]{1,0:T(8,128)(2,1)S(1)} %get-tuple-element.27), channel_id=1, source_target_pairs={{2,0},{3,1},{0,2},{1,3},{6,4},{7,5},{4,6},{5,7},{10,8},{11,9},{8,1... | collective-permute-start | bytes 196616 | tf_op jit(solution)/shard_map/ppermute | solution.py:20
  106.3 4.4 %collective-permute-start.18 = (bf16[64,512]{1,0:T(8,128)(2,1)S(1)}, bf16[64,512]{1,0:T(8,128)(2,1)S(1)}, u32[]{:S(2)}, u32[]{:S(2)}) collective-permute-start(bf16[64,512]{1,0:T(8,128)(2,1)S(1)} %get-tuple-element.27), channel_id=1, source_target_pairs={{1,0},{2,1},{3,2},{0,3},{5,4},{6,5},{7,6},{4,7},{9,8},{10,9},{11,1... | collective-permute-start | bytes 196616 | tf_op jit(solution)/shard_map/ppermute | solution.py:20
  110.8 8.9 %collective-permute-start.23 = (bf16[256,512]{1,0:T(8,128)(2,1)S(1)}, bf16[256,512]{1,0:T(8,128)(2,1)S(1)}, u32[]{:S(2)}, u32[]{:S(2)}) collective-permute-start(bf16[256,512]{1,0:T(8,128)(2,1)S(1)} %pad_maximum_fusion.4), channel_id=1, source_target_pairs={{192,0},{0,64},{64,128},{128,192},{193,1},{1,65},{65,129},{129,193... | collective-permute-start | bytes 786440 | tf_op jit(solution)/shard_map/ppermute | solution.py:20
  112.9 9.6 %collective-permute-start.22 = (bf16[256,512]{1,0:T(8,128)(2,1)S(1)}, bf16[256,512]{1,0:T(8,128)(2,1)S(1)}, u32[]{:S(2)}, u32[]{:S(2)}) collective-permute-start(bf16[256,512]{1,0:T(8,128)(2,1)S(1)} %pad_maximum_fusion.4), channel_id=1, source_target_pairs={{128,0},{192,64},{0,128},{64,192},{129,1},{193,65},{1,129},{65,193... | collective-permute-start | bytes 786440 | tf_op jit(solution)/shard_map/ppermute | solution.py:20
  114.6 8.1 %collective-permute-start.21 = (bf16[256,512]{1,0:T(8,128)(2,1)S(1)}, bf16[256,512]{1,0:T(8,128)(2,1)S(1)}, u32[]{:S(2)}, u32[]{:S(2)}) collective-permute-start(bf16[256,512]{1,0:T(8,128)(2,1)S(1)} %pad_maximum_fusion.4), channel_id=1, source_target_pairs={{64,0},{128,64},{192,128},{0,192},{65,1},{129,65},{193,129},{1,193... | collective-permute-start | bytes 786440 | tf_op jit(solution)/shard_map/ppermute | solution.py:20
  115.7 7.7 %copy-start.5 = (bf16[512,1792]{1,0:T(8,128)(2,1)S(1)}, bf16[512,1792]{1,0:T(8,128)(2,1)}, u32[]{:S(2)}) copy-start(bf16[512,1792]{1,0:T(8,128)(2,1)} %param.25) | copy-start | bytes 5505028
  123.4 1.5 copy-start.6
  125.7 1.8 copy-start.9
  125.7 1.7 copy-start.11
  125.8 1.7 copy-start.13
  125.8 1.7 copy-start.15
  125.8 1.7 copy-start.19
  125.8 5.9 %collective-permute-start.24 = (f32[128,3584]{1,0:T(8,128)S(1)}, f32[128,3584]{1,0:T(8,128)S(1)}, u32[]{:S(2)}, u32[]{:S(2)}) collective-permute-start(f32[128,3584]{1,0:T(8,128)S(1)} %pad_maximum_fusion), channel_id=1, source_target_pairs={{0,8},{8,0},{1,9},{9,1},{2,10},{10,2},{3,11},{11,3},{4,12},{12,4},... | collective-permute-start | bytes 5505032 | tf_op jit(solution)/shard_map/ppermute | solution.py:24
  126.9 4.1 %collective-permute-start.14 = (f32[128,1792]{1,0:T(8,128)S(1)}, f32[128,1792]{1,0:T(8,128)S(1)}, u32[]{:S(2)}, u32[]{:S(2)}) collective-permute-start(f32[128,1792]{1,0:T(8,128)S(1)} %fusion.51), channel_id=1, source_target_pairs={{0,8},{8,0},{1,9},{9,1},{2,10},{10,2},{3,11},{11,3},{4,12},{12,4},... | collective-permute-start | bytes 2752520 | tf_op jit(solution)/shard_map/ppermute | solution.py:24
  132.0 8.6 %collective-permute-start.27 = (bf16[32,3584]{1,0:T(8,128)(2,1)S(1)}, bf16[32,3584]{1,0:T(8,128)(2,1)S(1)}, u32[]{:S(2)}, u32[]{:S(2)}) collective-permute-start(bf16[32,3584]{1,0:T(8,128)(2,1)S(1)} %get-tuple-element.37), channel_id=1, source_target_pairs={{48,0},{0,16},{16,32},{32,48},{49,1},{1,17},{17,33},{33,49},{50,2}... | collective-permute-start | bytes 688136 | tf_op jit(solution)/shard_map/ppermute | solution.py:20
  132.1 25.6 %collective-permute-start.26 = (bf16[32,3584]{1,0:T(8,128)(2,1)S(1)}, bf16[32,3584]{1,0:T(8,128)(2,1)S(1)}, u32[]{:S(2)}, u32[]{:S(2)}) collective-permute-start(bf16[32,3584]{1,0:T(8,128)(2,1)S(1)} %get-tuple-element.38), channel_id=1, source_target_pairs={{32,0},{48,16},{0,32},{16,48},{33,1},{49,17},{1,33},{17,49},{34,2}... | collective-permute-start | bytes 688136 | tf_op jit(solution)/shard_map/ppermute | solution.py:20
  135.3 25.5 %collective-permute-start.25 = (bf16[32,3584]{1,0:T(8,128)(2,1)S(1)}, bf16[32,3584]{1,0:T(8,128)(2,1)S(1)}, u32[]{:S(2)}, u32[]{:S(2)}) collective-permute-start(bf16[32,3584]{1,0:T(8,128)(2,1)S(1)} %get-tuple-element.36), channel_id=1, source_target_pairs={{16,0},{32,16},{48,32},{0,48},{17,1},{33,17},{49,33},{1,49},{18,2}... | collective-permute-start | bytes 688136 | tf_op jit(solution)/shard_map/ppermute | solution.py:20
  135.4 25.5 %collective-permute-start.17 = (bf16[32,1792]{1,0:T(8,128)(2,1)S(1)}, bf16[32,1792]{1,0:T(8,128)(2,1)S(1)}, u32[]{:S(2)}, u32[]{:S(2)}) collective-permute-start(bf16[32,1792]{1,0:T(8,128)(2,1)S(1)} %get-tuple-element.46), channel_id=1, source_target_pairs={{48,0},{0,16},{16,32},{32,48},{49,1},{1,17},{17,33},{33,49},{50,2}... | collective-permute-start | bytes 344072 | tf_op jit(solution)/shard_map/ppermute | solution.py:20
  137.7 24.4 %collective-permute-start.16 = (bf16[32,1792]{1,0:T(8,128)(2,1)S(1)}, bf16[32,1792]{1,0:T(8,128)(2,1)S(1)}, u32[]{:S(2)}, u32[]{:S(2)}) collective-permute-start(bf16[32,1792]{1,0:T(8,128)(2,1)S(1)} %get-tuple-element.47), channel_id=1, source_target_pairs={{32,0},{48,16},{0,32},{16,48},{33,1},{49,17},{1,33},{17,49},{34,2}... | collective-permute-start | bytes 344072 | tf_op jit(solution)/shard_map/ppermute | solution.py:20
  140.6 25.0 %collective-permute-start.15 = (bf16[32,1792]{1,0:T(8,128)(2,1)S(1)}, bf16[32,1792]{1,0:T(8,128)(2,1)S(1)}, u32[]{:S(2)}, u32[]{:S(2)}) collective-permute-start(bf16[32,1792]{1,0:T(8,128)(2,1)S(1)} %get-tuple-element.45), channel_id=1, source_target_pairs={{16,0},{32,16},{48,32},{0,48},{17,1},{33,17},{49,33},{1,49},{18,2}... | collective-permute-start | bytes 344072 | tf_op jit(solution)/shard_map/ppermute | solution.py:20
  165.8 8.6 %collective-permute-start.30 = (bf16[32,3584]{1,0:T(8,128)(2,1)S(1)}, bf16[32,3584]{1,0:T(8,128)(2,1)S(1)}, u32[]{:S(2)}, u32[]{:S(2)}) collective-permute-start(bf16[32,3584]{1,0:T(8,128)(2,1)S(1)} %pad_maximum_fusion.7), channel_id=1, source_target_pairs={{48,0},{0,16},{16,32},{32,48},{49,1},{1,17},{17,33},{33,49},{50,2}... | collective-permute-start | bytes 688136 | tf_op jit(solution)/shard_map/ppermute | solution.py:20
  165.9 20.0 %collective-permute-start.29 = (bf16[32,3584]{1,0:T(8,128)(2,1)S(1)}, bf16[32,3584]{1,0:T(8,128)(2,1)S(1)}, u32[]{:S(2)}, u32[]{:S(2)}) collective-permute-start(bf16[32,3584]{1,0:T(8,128)(2,1)S(1)} %pad_maximum_fusion.7), channel_id=1, source_target_pairs={{32,0},{48,16},{0,32},{16,48},{33,1},{49,17},{1,33},{17,49},{34,2}... | collective-permute-start | bytes 688136 | tf_op jit(solution)/shard_map/ppermute | solution.py:20
  167.3 20.1 %collective-permute-start.28 = (bf16[32,3584]{1,0:T(8,128)(2,1)S(1)}, bf16[32,3584]{1,0:T(8,128)(2,1)S(1)}, u32[]{:S(2)}, u32[]{:S(2)}) collective-permute-start(bf16[32,3584]{1,0:T(8,128)(2,1)S(1)} %pad_maximum_fusion.7), channel_id=1, source_target_pairs={{16,0},{32,16},{48,32},{0,48},{17,1},{33,17},{49,33},{1,49},{18,2}... | collective-permute-start | bytes 688136 | tf_op jit(solution)/shard_map/ppermute | solution.py:20
  187.5 2.6 %collective-permute-start.31 = (bf16[128,3584]{1,0:T(8,128)(2,1)S(1)}, bf16[128,3584]{1,0:T(8,128)(2,1)S(1)}, u32[]{:S(2)}, u32[]{:S(2)}) collective-permute-start(bf16[128,3584]{1,0:T(8,128)(2,1)S(1)} %pad_maximum_fusion.1), channel_id=1, source_target_pairs={{0,8},{8,0},{1,9},{9,1},{2,10},{10,2},{3,11},{11,3},{4,12},{12,4},... | collective-permute-start | bytes 2752520 | tf_op jit(solution)/shard_map/ppermute | solution.py:24
  191.8 9.6 %collective-permute-start.34 = (bf16[256,512]{1,0:T(8,128)(2,1)S(1)}, bf16[256,512]{1,0:T(8,128)(2,1)S(1)}, u32[]{:S(2)}, u32[]{:S(2)}) collective-permute-start(bf16[256,512]{1,0:T(8,128)(2,1)S(1)} %convolution_convert_fusion), channel_id=1, source_target_pairs={{192,0},{0,64},{64,128},{128,192},{193,1},{1,65},{65,129},{129,193... | collective-permute-start | bytes 786440 | tf_op jit(solution)/shard_map/ppermute | solution.py:20
  193.9 9.3 %collective-permute-start.33 = (bf16[256,512]{1,0:T(8,128)(2,1)S(1)}, bf16[256,512]{1,0:T(8,128)(2,1)S(1)}, u32[]{:S(2)}, u32[]{:S(2)}) collective-permute-start(bf16[256,512]{1,0:T(8,128)(2,1)S(1)} %convolution_convert_fusion.1), channel_id=1, source_target_pairs={{64,0},{128,64},{192,128},{0,192},{65,1},{129,65},{193,129},{1,193... | collective-permute-start | bytes 786440 | tf_op jit(solution)/shard_map/ppermute | solution.py:20
  195.8 12.2 %collective-permute-start.32 = (bf16[256,512]{1,0:T(8,128)(2,1)S(1)}, bf16[256,512]{1,0:T(8,128)(2,1)S(1)}, u32[]{:S(2)}, u32[]{:S(2)}) collective-permute-start(bf16[256,512]{1,0:T(8,128)(2,1)S(1)} %convolution_convert_fusion.2), channel_id=1, source_target_pairs={{128,0},{192,64},{0,128},{64,192},{129,1},{193,65},{1,129},{65,193... | collective-permute-start | bytes 786440 | tf_op jit(solution)/shard_map/ppermute | solution.py:20
  220.9 8.3 %collective-permute-start.35 = (bf16[2,32,512]{2,1,0:T(8,128)(2,1)S(1)}, bf16[2,32,512]{2,1,0:T(8,128)(2,1)S(1)}, u32[]{:S(2)}, u32[]{:S(2)}) collective-permute-start(bf16[2,32,512]{2,1,0:T(8,128)(2,1)S(1)} %fusion.76), channel_id=1, source_target_pairs={{0,4},{4,0},{1,5},{5,1},{2,6},{6,2},{3,7},{7,3},{8,12},{12,8},{9,1... | collective-permute-start | bytes 196616 | tf_op jit(solution)/shard_map/ppermute | solution.py:24
